TPU v7x, 128 devices: a whole 4x4x4 slice. The times are simulated.
128 devices in a mesh: tm: 16 (over z, x_hi, core), space: 8 (over x_lo, y).
Axes of the slice: x: 4 (x_hi: 2, x_lo: 2; x = x_hi * 2 + x_lo), y: 4, z: 4, core: 2. Of those that a mesh axis runs over, the one named last changes fastest.
Arguments:
- solution: float32 [512, 384, 384], P('tm', 'space'), may hold values from -6 to 6
- residual: float32 [512, 384, 384], P('tm', 'space'), may hold values from -6 to 6
- direction: float32 [512, 384, 384], P('tm', 'space'), may hold values from -6 to 6
- reaction: float32 [512, 384, 384], P('tm', 'space'), may hold values from 0.1 to 2
- time_bands: float32 [2, 4, 512], replicated, may hold values from -0.25 to 1.1, as said below
- space_bands: float32 [2, 4, 384], replicated, may hold values from -0.25 to 1.1, as said below
- time_basis: float32 [512, 512], replicated, may hold values from -0.25 to 0.25
- space_basis: float32 [384, 384], replicated, may hold values from -0.3125 to 0.3125
- time_eigen: float32 [512], replicated, may hold values from 0.1 to 1
- space_eigen: float32 [384], replicated, may hold values from 0.1 to 1
Outputs:
- new_solution: float32 [512, 384, 384], P('tm', 'space')
- new_residual: float32 [512, 384, 384], P('tm', 'space')
- new_direction: float32 [512, 384, 384], P('tm', 'space')
Inputs may be any that keep to these rules, and one draw needn't show every extreme that they name: `time_bands`: each of the two matrices is symmetric with every diagonal entry larger than the sum of the magnitudes of the other entries of its row. `space_bands`: each of the two matrices is symmetric with every diagonal entry larger than the sum of the magnitudes of the other entries of its row.
All inputs are finite; a program needn't handle non-finite values.
Results may differ from a plain program's by a relative error of at most 0.000051.
Values sent between devices are 32-bit elements; how exact they have to be, the bound alone decides.
A program may use at most 128 MiB of HBM per device.

v0:
```python
import jax
import jax.numpy as jnp
from jax import lax
from jax.sharding import Mesh
from jax.sharding import PartitionSpec as P

TM_SPACE = ("tm_0", "tm_1", "tm_2", "space_0", "space_1")
TM = ("tm_0", "tm_1", "tm_2")
SPACE = ("space_0", "space_1")


highest = lax.Precision.HIGHEST


def extended_2(cells, sides, width):
    for axis, dim in sides:
        count = lax.axis_size(axis)
        ends = count - 1
        head = lax.slice_in_dim(cells, 0, width, axis=dim)
        tail = lax.slice_in_dim(cells, cells.shape[dim] - width, cells.shape[dim], axis=dim)
        cells = jnp.concatenate(
            [
                lax.ppermute(tail, axis, [(i, (i + 1) % count) for i in range(ends)]),
                cells,
                lax.ppermute(head, axis, [((i + 1) % count, i) for i in range(ends)]),
            ],
            axis=dim,
        )
    return cells


def cut_along(shard, dim, count):
    before, after = (shard.shape[:dim], shard.shape[dim + 1 :])
    return jnp.moveaxis(shard.reshape(*before, count, -1, *after), dim, 0)


def joined_along(pieces, dim):
    lengths = list(pieces.shape[1:])
    lengths[dim] *= pieces.shape[0]
    return jnp.moveaxis(pieces, 0, dim).reshape(lengths)


def exchange_in_order(pieces, axes, turns):
    lengths = [lax.axis_size(a) for a in axes]
    pieces = pieces.reshape(*lengths, *pieces.shape[1:])
    for k in turns:
        pieces = lax.all_to_all(pieces, axes[k], split_axis=k, concat_axis=k, tiled=True)
    return pieces.reshape(-1, *pieces.shape[len(axes) :])


def two_step_exchange(shard, groups, turns, split_dim, concat_dim):
    count = lax.axis_size(groups[0]) * lax.axis_size(groups[1])
    pieces = cut_along(shard, split_dim, count)
    return joined_along(exchange_in_order(pieces, groups, turns), concat_dim)


def over_axes(shard, axes):
    for axis in axes:
        shard = lax.psum(shard, axis)
    return shard


def band_apply(extended, band_rows, dimension):
    length = extended.shape[dimension] - 6
    target_shape = [1] * extended.ndim
    target_shape[dimension] = length

    def coefficient(which_row, first_row):
        return lax.slice_in_dim(band_rows[which_row], first_row, first_row + length).reshape(
            target_shape
        )

    def window(first_row):
        return lax.slice_in_dim(extended, first_row, first_row + length, axis=dimension)

    result = coefficient(0, 3) * window(3)
    for offset in (1, 2, 3):
        result = (
            result
            + coefficient(offset, 3) * window(3 + offset)
            + coefficient(offset, 3 - offset) * window(3 - offset)
        )
    return result


def pad_along(values, dimension):
    widths = [(0, 0)] * values.ndim
    widths[dimension] = (3, 3)
    return jnp.pad(values, widths)


def apply_operator(direction, reaction, time_bands, space_bands):
    rows_time = direction.shape[0]
    rows_space = direction.shape[1]
    halo_block = extended_2(direction, ((TM, 0), (SPACE, 1)), 3)
    padded_time = jnp.pad(time_bands, ((0, 0), (0, 0), (3, 3)))
    padded_space = jnp.pad(space_bands, ((0, 0), (0, 0), (3, 3)))
    time_rows = lax.dynamic_slice_in_dim(
        padded_time, lax.axis_index(TM) * rows_time, rows_time + 6, 2
    )
    space_rows = lax.dynamic_slice_in_dim(
        padded_space, lax.axis_index(SPACE) * rows_space, rows_space + 6, 2
    )
    extended = pad_along(halo_block, 2)
    mass_y = band_apply(extended, padded_space[1], 2)
    stiff_y = band_apply(extended, padded_space[0], 2)
    mass_xy = band_apply(mass_y, space_rows[1], 1)
    stiff_x = band_apply(mass_y, space_rows[0], 1)
    stiff_yx = band_apply(stiff_y, space_rows[1], 1)
    temporal = band_apply(mass_xy, time_rows[0], 0) + band_apply(
        stiff_x + stiff_yx, time_rows[1], 0
    )
    return temporal + reaction * direction


def spectrum(time_eigen, space_eigen):
    time_count = lax.axis_size(TM)
    space_count = lax.axis_size(SPACE)
    block_width = space_eigen.shape[0] // (time_count * space_count)
    group_index = lax.axis_index(SPACE) * time_count + lax.axis_index(TM)
    block = lax.dynamic_slice_in_dim(space_eigen, group_index * block_width, block_width)
    return time_eigen[:, None, None] + space_eigen[None, :, None] + block[None, None, :]


def forward_fields(fields, time_basis, space_basis):
    along_y = jnp.einsum("ctxk,ka->ctxa", fields, space_basis, precision=highest)
    spread = lax.all_to_all(along_y, SPACE, split_axis=3, concat_axis=2, tiled=True)
    along_x = jnp.einsum("ctjy,jb->ctby", spread, space_basis, precision=highest)
    joined = lax.all_to_all(along_x, TM, split_axis=3, concat_axis=1, tiled=True)
    return jnp.einsum("cixy,ia->caxy", joined, time_basis, precision=highest)


def inverse_fields(spectral, time_basis, space_basis):
    along_t = jnp.einsum("caxy,ia->cixy", spectral, time_basis, precision=highest)
    parted = two_step_exchange(along_t, (("tm_0", "tm_1"), "tm_2"), (1, 0), 1, 3)
    along_x = jnp.einsum("ctby,jb->ctjy", parted, space_basis, precision=highest)
    blocks = lax.all_to_all(along_x, SPACE, split_axis=2, concat_axis=3, tiled=True)
    return jnp.einsum("ctxa,ka->ctxk", blocks, space_basis, precision=highest)


def per_device(
    solution,
    residual,
    direction,
    reaction,
    time_bands,
    space_bands,
    time_basis,
    space_basis,
    time_eigen,
    space_eigen,
):
    image = apply_operator(direction, reaction, time_bands, space_bands)
    eigen_sum = spectrum(time_eigen, space_eigen)
    both_hat = forward_fields(jnp.stack([residual, image]), time_basis, space_basis)
    first_scaled = both_hat[0] / eigen_sum
    image_scaled = both_hat[1] / eigen_sum
    norm_old, cross_term, image_norm, curvature = (
        over_axes(jnp.sum(both_hat[0] * first_scaled), TM_SPACE),
        over_axes(jnp.sum(both_hat[1] * first_scaled), TM_SPACE),
        over_axes(jnp.sum(both_hat[1] * image_scaled), TM_SPACE),
        over_axes(jnp.sum(direction * image), TM_SPACE),
    )
    step_size = norm_old / curvature
    new_residual = residual - step_size * image
    spectral = first_scaled - step_size * image_scaled
    norm_new = norm_old - 2.0 * step_size * cross_term + step_size * step_size * image_norm
    precond = inverse_fields(spectral[None], time_basis, space_basis)[0]
    new_direction = precond + norm_new / norm_old * direction
    new_solution = solution + step_size * direction
    return (new_solution, new_residual, new_direction)


def solution(mesh):
    finer = Mesh(
        mesh.devices.reshape(4, 2, 2, 2, 4), ("tm_0", "tm_1", "tm_2", "space_0", "space_1")
    )
    in_specs = (
        P(TM, SPACE, None),
        P(TM, SPACE, None),
        P(TM, SPACE, None),
        P(TM, SPACE, None),
        P(),
        P(),
        P(),
        P(),
        P(),
        P(),
    )
    out_specs = (P(TM, SPACE, None), P(TM, SPACE, None), P(TM, SPACE, None))
    return jax.shard_map(
        per_device, mesh=finer, in_specs=in_specs, out_specs=out_specs, check_vma=False
    )
```

profile of v0, /device:TPU:1, one launch (start us, length us, event | category | flops | bytes accessed | tf_op | source)
XLA Modules:
  0.0 526.5 jit_solution(127195260726409566)
XLA Ops:
  1.8 6.0 %collective-permute-start = (f32[3,48,384]{2,1,0:T(8,128)S(1)}, f32[3,48,384]{2,1,0:T(8,128)S(1)}, u32[]{:S(2)}, u32[]{:S(2)}) collective-permute-start(f32[3,48,384]{2,1,0:T(8,128)S(1)} %get-tuple-element.47), channel_id=1, source_target_pairs={{0,8},{8,16},{16,24},{24,32},{32,40},{40,48},{48,56},{56,64},{64,7... | collective-permute-start | bytes 663560 | tf_op jit(solution)/shard_map/ppermute | solution.py:23
  7.8 1.9 collective-permute-start.1
  12.9 1.8 constant_dynamic-update-slice_fusion.1
  14.7 1.9 collective-permute-done.1
  16.7 3.2 collective-permute-start.2
  21.5 1.4 collective-permute-done.2
  22.9 3.8 collective-permute-done.3
  26.7 2.1 pad_maximum_fusion
  28.8 30.2 %multiply_add_fusion.1 = (f32[38,54,384]{2,1,0:T(8,128)}, f32[38,54,384]{2,1,0:T(8,128)}) fusion(f32[38,54,384]{2,1,0:T(8,128)} %pad_maximum_fusion, f32[384]{0:T(512)S(1)} %get-tuple-element.9, f32[384]{0:T(512)S(1)} %get-tuple-element.15, f32[384]{0:T(512)S(1)} %get-tuple-element.8, f32[384]{0:T(512)S(1)} %get-tuple-element.16, ...), kind=kLoop, calls=%fused_computation.18 | loop fusion | flops 20487168 | bytes 9477120 | tf_op jit(solution)/shard_map/add | solution.py:79
  59.0 12.2 %multiply_add_fusion.2 = f32[38,48,384]{2,1,0:T(8,128)} fusion(f32[38,54,384]{2,1,0:T(8,128)} %get-tuple-element.42, f32[48]{0:T(128)S(1)} %get-tuple-element.70, f32[48]{0:T(128)S(1)} %get-tuple-element.71, f32[48]{0:T(128)S(1)} %get-tuple-element.72, f32[48]{0:T(128)S(1)} %get-tuple-element.73, f32[48]{0:T(128)S(1)} %get-tuple-element.75, ...), kind=kLoop, calls=%fused_computation.33 | loop fusion | flops 9105408 | bytes 22414656 | tf_op jit(solution)/shard_map/add | solution.py:79
  71.2 5.8 %fusion.5 = f32[38,48,384]{2,1,0:T(8,128)} fusion(f32[38,54,384]{2,1,0:T(8,128)S(1)} %copy-done.2, f32[38,54,384]{2,1,0:T(8,128)S(1)} %copy-done.1, f32[48]{0:T(128)S(1)} %get-tuple-element.64, f32[48]{0:T(128)S(1)} %get-tuple-element.65, f32[48]{0:T(128)S(1)} %get-tuple-element.63, f32[48]{0:T(128)S(1)} %get-tuple-element.66, f32[48]{0:T(128)S(1)} %get-tuple-element.68, ...), kind=kLoop, calls=%fused_computation.21 | loop fusion | flops 18911232 | bytes 42027648 | tf_op jit(solution)/shard_map/add | solution.py:111
  77.1 16.6 %multiply_reduce_fusion = (f32[]{:T(128)}, f32[32,48,384]{2,1,0:T(8,128)S(1)}) fusion(f32[32,48,384]{2,1,0:T(8,128)} %param.12, f32[32,48,384]{2,1,0:T(8,128)} %param.13, f32[38,48,384]{2,1,0:T(8,128)} %fusion.5, f32[32]{0:T(128)S(1)} %get-tuple-element.54, f32[32]{0:T(128)S(1)} %get-tuple-element.55, f32[32]{0:T(128)S(1)} %get-tuple-element.53, ...), kind=kLoop, calls=%fused_computation.75 | loop fusion | flops 18284544 | bytes 40109828 | tf_op jit(solution)/shard_map/reduce_sum | solution.py:162
  93.7 1.4 copy-done.4
  95.1 10.6 %fusion = f32[2,32,48,384]{3,2,1,0:T(8,128)} fusion(f32[1,32,48,384]{3,2,1,0:T(8,128)S(1)} %bitcast.155, f32[1,32,48,384]{3,2,1,0:T(8,128)S(1)} %bitcast.157, f32[384,384]{1,0:T(8,128)S(1)} %copy-done.7), kind=kOutput, calls=%fused_computation.8 | convolution fusion | flops 5436997632 | bytes 10027008 | tf_op jit(solution)/shard_map/ctxk,ka->ctxa/dot_general | solution.py:126
  105.7 12.0 %copy.26 = f32[2,32,48,384]{2,1,0,3:T(8,128)} copy(f32[2,32,48,384]{3,2,1,0:T(8,128)} %fusion) | data formatting | bytes 9437184 | tf_op jit(solution)/shard_map/ctxk,ka->ctxa/dot_general | solution.py:126
  117.8 14.4 %reshape.301 = f32[8,1,147456]{2,1,0:T(1,128)} reshape(f32[384,2,32,48]{3,2,1,0:T(8,128)} %bitcast.151) | data formatting | bytes 9437184
  132.2 57.9 %all_to_all.61 = f32[8,1,147456]{2,1,0:T(1,128)} all-to-all(f32[8,1,147456]{2,1,0:T(1,128)} %reshape.301), channel_id=1, replica_groups=mesh['tm_0'=4,'tm_1'=2,'tm_2'=2,'space_0'=2,'space_1'=4] {'space_0','spa..., dimensions={0} | all-to-all | bytes 9437184 | tf_op jit(solution)/shard_map/all_to_all | solution.py:127
  190.5 15.9 %reduce.28 = f32[8,147456]{1,0:T(8,128)} reduce(f32[8,1,147456]{2,1,0:T(1,128)} %all_to_all.61, f32[]{:T(128)} %broadcast.59), dimensions={1}, to_apply=%all_to_all.43.reduce_sub_computation | reduce | bytes 9437188 | tf_op jit(solution)/shard_map/all_to_all | solution.py:127
  206.4 11.9 %reshape.302 = f32[384,2,32,48]{3,2,1,0:T(8,128)} reshape(f32[8,147456]{1,0:T(8,128)} %reduce.28) | data formatting | bytes 9437184
  218.4 16.7 %copy.52 = f32[2,32,48,8,48]{2,3,4,1,0:T(8,128)} copy(f32[2,32,48,8,48]{2,1,0,4,3:T(8,128)} %bitcast.149) | data formatting | bytes 9437184 | tf_op jit(solution)/shard_map/all_to_all | solution.py:127
  235.1 10.7 %all_to_all.46 = f32[2,32,384,48]{2,3,1,0:T(8,128)} reshape(f32[2,32,8,48,48]{3,2,4,1,0:T(8,128)} %bitcast.150) | data formatting | bytes 9437184 | tf_op jit(solution)/shard_map/all_to_all | solution.py:127
  245.8 11.8 %convolution_bitcast_fusion = f32[2,32,384,48]{2,3,1,0:T(8,128)S(1)} fusion(f32[2,32,384,48]{2,3,1,0:T(8,128)} %all_to_all.46, f32[384,384]{1,0:T(8,128)S(1)} %copy-done.7), kind=kOutput, calls=%fused_computation.77 | convolution fusion | flops 5435817984 | bytes 10027008 | tf_op jit(solution)/shard_map/ctjy,jb->ctby/dot_general | solution.py:128
  257.6 3.6 copy.28
  261.2 13.3 %all-to-all-start.1 = ((f32[2,32,384,48]{2,1,0,3:T(8,128)}), f32[2,32,384,48]{2,1,0,3:T(8,128)}, u32[]{:S(2)}, u32[]{:S(2)}) async-start(f32[2,32,384,48]{2,1,0,3:T(8,128)} %copy.28), calls=%async_computation.1 | async-start | bytes 9437184 | tf_op jit(solution)/shard_map/all_to_all | solution.py:129
  274.7 56.2 %all-to-all-done.1 = f32[2,32,384,48]{2,1,0,3:T(8,128)} async-done(((f32[2,32,384,48]{2,1,0,3:T(8,128)}), f32[2,32,384,48]{2,1,0,3:T(8,128)}, u32[]{:S(2)}, u32[]{:S(2)}) %all-to-all-start.1) | async-done | bytes 4718624 | tf_op jit(solution)/shard_map/all_to_all | solution.py:129
  330.8 2.8 copy.30
  333.7 8.0 %convolution_bitcast_fusion.1 = f32[2,512,384,3]{1,2,3,0:T(8,128)S(1)} fusion(f32[2,512,384,3]{2,1,3,0:T(8,128)S(1)} %bitcast.156, f32[512,512]{1,0:T(8,128)S(1)} %copy-done), kind=kOutput, calls=%fused_computation.78 | convolution fusion | flops 7247757312 | bytes 10485760 | tf_op jit(solution)/shard_map/cixy,ia->caxy/dot_general | solution.py:130
  341.7 2.1 copy-done.5
  343.8 2.2 fusion.35
  346.0 7.9 %all-reduce.4 = (f32[]{:T(128)}, f32[]{:T(128)}, f32[]{:T(128)}, f32[]{:T(128)}) all-reduce(f32[]{:T(128)} %get-tuple-element.5, f32[]{:T(128)} %get-tuple-element.40, f32[]{:T(128)} %get-tuple-element.4, f32[]{:T(128)} %get-tuple-element.3), channel_id=1, replica_groups=mesh['tm_0'=4,'tm_1'=2,'tm_2'=2,'space_0'=2,'space_1'=4] {'tm_0'}, use_global_device_ids=true, to_apply=%region_1.2 | all-reduce | flops 4 | bytes 32 | tf_op jit(solution)/shard_map/psum | solution.py:59
  353.9 6.0 %all-reduce.7 = (f32[]{:T(128)}, f32[]{:T(128)}, f32[]{:T(128)}, f32[]{:T(128)}) all-reduce(f32[]{:T(128)} %get-tuple-element.24, f32[]{:T(128)} %get-tuple-element.25, f32[]{:T(128)} %get-tuple-element.26, f32[]{:T(128)} %get-tuple-element.27), channel_id=1, replica_groups=mesh['tm_0'=4,'tm_1'=2,'tm_2'=2,'space_0'=2,'space_1'=4] {'tm_1'}, use_global_device_ids=true, to_apply=%region_2.3 | all-reduce | flops 4 | bytes 32 | tf_op jit(solution)/shard_map/psum | solution.py:59
  359.9 7.0 %all-reduce.6 = (f32[]{:T(128)}, f32[]{:T(128)}, f32[]{:T(128)}, f32[]{:T(128)}) all-reduce(f32[]{:T(128)} %get-tuple-element.36, f32[]{:T(128)} %get-tuple-element.37, f32[]{:T(128)} %get-tuple-element.38, f32[]{:T(128)} %get-tuple-element.39), channel_id=1, replica_groups=mesh['tm_0'=4,'tm_1'=2,'tm_2'=2,'space_0'=2,'space_1'=4] {'tm_2'}, use_global_device_ids=true, to_apply=%region_3.4 | all-reduce | flops 4 | bytes 32 | tf_op jit(solution)/shard_map/psum | solution.py:59
  366.9 4.5 all-reduce.5
  371.4 7.6 %all-reduce.3 = (f32[]{:T(128)}, f32[]{:T(128)}, f32[]{:T(128)}, f32[]{:T(128)}) all-reduce(f32[]{:T(128)} %get-tuple-element.28, f32[]{:T(128)} %get-tuple-element.29, f32[]{:T(128)} %get-tuple-element.30, f32[]{:T(128)} %get-tuple-element.31), channel_id=1, replica_groups=mesh['tm_0'=4,'tm_1'=2,'tm_2'=2,'space_0'=2,'space_1'=4] {'space_1'}, use_global_device_ids=true, to_apply=%region_5.6 | all-reduce | flops 4 | bytes 32 | tf_op jit(solution)/shard_map/psum | solution.py:59
  380.3 7.2 %fusion.38 = f32[8,2,1,32,384,3]{4,3,1,0,5,2:T(8,128)S(1)} fusion(f32[8,2,32,512,1]{3,2,1,0,4:T(8,128)S(1)} %bitcast.148, f32[2,512,384,3]{1,2,3,0:T(8,128)} %copy-done.5, f32[]{:T(128)S(6)} %div.19, f32[3]{0:T(128)S(1)} %dynamic_slice.11, f32[512,384]{0,1:T(8,128)S(1)} %broadcast_add_fusion), kind=kOutput, calls=%fused_computation.81 | convolution fusion | flops 3626827776 | bytes 8912912 | tf_op jit(solution)/shard_map/caxy,ia->cixy/dot_general | solution.py:134
  387.7 8.8 %all_to_all.62 = f32[8,2,1,32,384,3]{4,3,0,5,2,1:T(8,128)S(1)} all-to-all(f32[8,2,1,32,384,3]{4,3,0,5,2,1:T(8,128)S(1)} %copy.33), channel_id=1, replica_groups=mesh['tm_0'=4,'tm_1'=2,'tm_2'=2,'space_0'=2,'space_1'=4] {'tm_2'}, dimensions={1} | all-to-all | bytes 4718592 | tf_op jit(solution)/shard_map/all_to_all | solution.py:47
  396.7 33.4 %all_to_all.63 = f32[8,2,1,32,384,3]{4,3,1,5,2,0:T(8,128)S(1)} all-to-all(f32[8,2,1,32,384,3]{4,3,1,5,2,0:T(8,128)S(1)} %copy.34), channel_id=1, replica_groups=mesh['tm_0'=4,'tm_1'=2,'tm_2'=2,'space_0'=2,'space_1'=4] {'tm_0','tm_1'}, dimensions={0} | all-to-all | bytes 4718592 | tf_op jit(solution)/shard_map/all_to_all | solution.py:47
  430.3 7.2 %fusion.41 = f32[1,32,384,48]{2,3,1,0:T(8,128)} fusion(f32[32,384,48]{1,0,2:T(8,128)S(1)} %bitcast.158, f32[384,384]{1,0:T(8,128)S(1)} %copy-done.7), kind=kOutput, calls=%fused_computation.82 | convolution fusion | flops 2717908992 | bytes 5308416 | tf_op jit(solution)/shard_map/ctby,jb->ctjy/dot_general | solution.py:136
  437.5 7.2 %copy.37 = f32[1,32,384,48]{3,1,0,2:T(8,128)} copy(f32[1,32,384,48]{2,3,1,0:T(8,128)} %fusion.41) | data formatting | bytes 4718592 | tf_op jit(solution)/shard_map/ctby,jb->ctjy/transpose | solution.py:136
  444.7 9.5 %reshape.303 = f32[8,1,73728]{2,1,0:T(1,128)} reshape(f32[384,1,32,48]{3,2,1,0:T(8,128)} %bitcast.154) | data formatting | bytes 4718592
  454.2 4.7 all-to-all-start.4
  461.4 5.8 %multiply_subtract_fusion = (f32[32,48,384]{2,1,0:T(8,128)}, f32[32,48,384]{2,1,0:T(8,128)}) fusion(f32[32,48,384]{2,1,0:T(8,128)} %param.11, f32[32,48,384]{2,1,0:T(8,128)} %copy-done.4, f32[]{:T(128)S(6)} %div.19, f32[32,48,384]{2,1,0:T(8,128)} %param.10, f32[32,48,384]{2,1,0:T(8,128)S(1)} %copy-done.3), kind=kLoop, calls=%fused_computation.73 | loop fusion | flops 2359296 | bytes 14155780 | tf_op jit(solution)/shard_map/sub | solution.py:165
  467.2 20.5 %all-to-all-done.4 = f32[8,1,73728]{2,1,0:T(1,128)} async-done(((f32[8,1,73728]{2,1,0:T(1,128)}), f32[8,1,73728]{2,1,0:T(1,128)}, u32[]{:S(2)}, u32[]{:S(2)}) %all-to-all-start.4) | async-done | bytes 2359328 | tf_op jit(solution)/shard_map/all_to_all | solution.py:137
  487.7 9.3 %reduce.29 = f32[8,73728]{1,0:T(8,128)} reduce(f32[8,1,73728]{2,1,0:T(1,128)} %all-to-all-done.4, f32[]{:T(128)} %broadcast.59), dimensions={1}, to_apply=%all_to_all.53.reduce_sub_computation | reduce | bytes 4718596 | tf_op jit(solution)/shard_map/all_to_all | solution.py:137
  497.0 6.9 %reshape.304 = f32[384,1,32,48]{3,2,1,0:T(8,128)} reshape(f32[8,73728]{1,0:T(8,128)} %reduce.29) | data formatting | bytes 4718592
  503.9 9.3 %copy.53 = f32[1,32,8,48,48]{4,2,3,1,0:T(8,128)} copy(f32[1,32,8,48,48]{4,1,3,2,0:T(8,128)} %bitcast.152) | data formatting | bytes 4718592 | tf_op jit(solution)/shard_map/all_to_all | solution.py:137
  513.2 5.9 %reshape.281 = f32[32,48,384]{2,1,0:T(8,128)} reshape(f32[1,32,48,8,48]{4,3,2,1,0:T(8,128)} %bitcast.153) | data formatting | bytes 4718592 | tf_op jit(solution)/shard_map/reshape.193
  519.1 7.2 %multiply_add_fusion.3 = f32[32,48,384]{2,1,0:T(8,128)} fusion(f32[32,48,384]{2,1,0:T(8,128)S(1)} %copy-done.3, f32[32,48,384]{2,1,0:T(8,128)} %reshape.281, f32[]{:T(128)S(6)} %div.23, f32[384,384]{1,0:T(8,128)} %param.17), kind=kOutput, calls=%fused_computation.72 | convolution fusion | flops 2719088640 | bytes 7667716 | tf_op jit(solution)/shard_map/ctxa,ka->ctxk/dot_general | solution.py:138
  (39 shorter events, 7.1 us)
Async XLA Ops:
  0.6 333.0 %copy-start = (f32[512,512]{1,0:T(8,128)S(1)}, f32[512,512]{1,0:T(8,128)}, u32[]{:S(2)}) copy-start(f32[512,512]{1,0:T(8,128)} %param.16) | copy-start | bytes 3145732
  1.8 11.0 %collective-permute-start = (f32[3,48,384]{2,1,0:T(8,128)S(1)}, f32[3,48,384]{2,1,0:T(8,128)S(1)}, u32[]{:S(2)}, u32[]{:S(2)}) collective-permute-start(f32[3,48,384]{2,1,0:T(8,128)S(1)} %get-tuple-element.47), channel_id=1, source_target_pairs={{0,8},{8,16},{16,24},{24,32},{32,40},{40,48},{48,56},{56,64},{64,7... | collective-permute-start | bytes 663560 | tf_op jit(solution)/shard_map/ppermute | solution.py:23
  7.8 8.8 %collective-permute-start.1 = (f32[3,48,384]{2,1,0:T(8,128)S(1)}, f32[3,48,384]{2,1,0:T(8,128)S(1)}, u32[]{:S(2)}, u32[]{:S(2)}) collective-permute-start(f32[3,48,384]{2,1,0:T(8,128)S(1)} %get-tuple-element.46), channel_id=1, source_target_pairs={{8,0},{16,8},{24,16},{32,24},{40,32},{48,40},{56,48},{64,56},{72,6... | collective-permute-start | bytes 663560 | tf_op jit(solution)/shard_map/ppermute | solution.py:25
  12.8 8.4 %copy-start.9 = (f32[2,4,512]{2,1,0:T(4,128)S(1)}, f32[2,4,512]{2,1,0:T(4,128)}, u32[]{:S(2)}) copy-start(f32[2,4,512]{2,1,0:T(4,128)} %param.14) | copy-start | bytes 49156
  12.8 8.5 %copy-start.8 = (f32[2,4,384]{2,1,0:T(4,128)S(1)}, f32[2,4,384]{2,1,0:T(4,128)}, u32[]{:S(2)}) copy-start(f32[2,4,384]{2,1,0:T(4,128)} %param.15) | copy-start | bytes 36868
  16.7 6.2 %collective-permute-start.2 = (f32[38,3,384]{2,1,0:T(4,128)S(1)}, f32[38,3,384]{2,1,0:T(4,128)S(1)}, u32[]{:S(2)}, u32[]{:S(2)}) collective-permute-start(f32[38,3,384]{2,1,0:T(4,128)S(1)} %get-tuple-element.44), channel_id=1, source_target_pairs={{0,1},{1,2},{2,3},{3,4},{4,5},{5,6},{6,7},{8,9},{9,10},{10,11},{11... | collective-permute-start | bytes 525320 | tf_op jit(solution)/shard_map/ppermute | solution.py:23
  19.9 6.8 %collective-permute-start.3 = (f32[38,3,384]{2,1,0:T(4,128)S(1)}, f32[38,3,384]{2,1,0:T(4,128)S(1)}, u32[]{:S(2)}, u32[]{:S(2)}) collective-permute-start(f32[38,3,384]{2,1,0:T(4,128)S(1)} %get-tuple-element.45), channel_id=1, source_target_pairs={{1,0},{2,1},{3,2},{4,3},{5,4},{6,5},{7,6},{9,8},{10,9},{11,10},{12... | collective-permute-start | bytes 525320 | tf_op jit(solution)/shard_map/ppermute | solution.py:25
  59.0 12.2 %copy-start.1 = (f32[38,54,384]{2,1,0:T(8,128)S(1)}, f32[38,54,384]{2,1,0:T(8,128)}, u32[]{:S(2)}) copy-start(f32[38,54,384]{2,1,0:T(8,128)} %get-tuple-element.42) | copy-start | bytes 9455620
  59.0 12.2 %copy-start.2 = (f32[38,54,384]{2,1,0:T(8,128)S(1)}, f32[38,54,384]{2,1,0:T(8,128)}, u32[]{:S(2)}) copy-start(f32[38,54,384]{2,1,0:T(8,128)} %get-tuple-element.43) | copy-start | bytes 9455620
  77.1 18.0 %copy-start.6 = (f32[32,48,384]{2,1,0:T(8,128)S(1)}, f32[32,48,384]{2,1,0:T(8,128)}, u32[]{:S(2)}) copy-start(f32[32,48,384]{2,1,0:T(8,128)} %param.11) | copy-start | bytes 7077892
  77.1 18.0 %copy-start.7 = (f32[384,384]{1,0:T(8,128)S(1)}, f32[384,384]{1,0:T(8,128)}, u32[]{:S(2)}) copy-start(f32[384,384]{1,0:T(8,128)} %param.17) | copy-start | bytes 1769476
  93.7 1.4 copy-start.4
  261.2 13.3 %copy-start.10 = (f32[384]{0:T(512)S(1)}, f32[384]{0:T(512)}, u32[]{:S(2)}) copy-start(f32[384]{0:T(512)} %param.19) | copy-start | bytes 4612
  261.2 13.4 %copy-start.11 = (f32[512]{0:T(512)S(1)}, f32[512]{0:T(512)}, u32[]{:S(2)}) copy-start(f32[512]{0:T(512)} %param.18) | copy-start | bytes 6148
  261.2 69.7 %all-to-all-start.1 = ((f32[2,32,384,48]{2,1,0,3:T(8,128)}), f32[2,32,384,48]{2,1,0,3:T(8,128)}, u32[]{:S(2)}, u32[]{:S(2)}) async-start(f32[2,32,384,48]{2,1,0,3:T(8,128)} %copy.28), calls=%async_computation.1 | async-start | bytes 9437184 | tf_op jit(solution)/shard_map/all_to_all | solution.py:129
  341.7 2.1 copy-start.5
  454.2 7.2 %copy-start.3 = (f32[32,48,384]{2,1,0:T(8,128)S(1)}, f32[32,48,384]{2,1,0:T(8,128)}, u32[]{:S(2)}) copy-start(f32[32,48,384]{2,1,0:T(8,128)} %param.12) | copy-start | bytes 7077892
  454.2 33.5 %all-to-all-start.4 = ((f32[8,1,73728]{2,1,0:T(1,128)}), f32[8,1,73728]{2,1,0:T(1,128)}, u32[]{:S(2)}, u32[]{:S(2)}) async-start(f32[8,1,73728]{2,1,0:T(1,128)} %reshape.303), calls=%async_computation.4 | async-start | bytes 4718592 | tf_op jit(solution)/shard_map/all_to_all | solution.py:137
where the time goes:
time: 537 us; the launch traced here: 526 us
  blocking collectives  133 us (25%)
  local copies, waits for them, and re-layouts  122 us (23%)
  other arithmetic  100 us (19%)
  waiting for transfers between devices  83.8 us (16%)
  matrix products  52 us (10%)
  starting transfers between devices  30.4 us (6%)
    all_to_all x1, blocking collectives, forward_fields(): lax.all_to_all(along_y, SPACE, split_axis=3, concat_axis=2, tiled=True)  57.9 us
    all_to_all x1, waiting for transfers between devices, forward_fields(): lax.all_to_all(along_x, TM, split_axis=3, concat_axis=1, tiled=True)  56.2 us
    unnamed x30, local copies, waits for them, and re-layouts  48.1 us
    add x2, other arithmetic, band_apply(): result + coefficient(offset, 3) * window(3 + offset)  42.4 us
    all_to_all x2, blocking collectives, exchange_in_order(): lax.all_to_all(pieces, axes[k], split_axis=k, concat_axis=k, tiled=True)  42.2 us
    psum x5, blocking collectives, over_axes(): shard = lax.psum(shard, axis)  33 us
    all_to_all x3, local copies, waits for them, and re-layouts, forward_fields(): lax.all_to_all(along_y, SPACE, split_axis=3, concat_axis=2, tiled=True)  27.9 us
    all_to_all x1, waiting for transfers between devices, inverse_fields(): lax.all_to_all(along_x, SPACE, split_axis=2, concat_axis=3, tiled=True)  20.5 us
  transfers between devices with their start and end apart: 6, of which 5 were waited for; matrix products, arithmetic and copies ran while one was open for 2% of the time, Pallas kernels for 0%

commit v1 on v0

v1 whole, which is shorter than its diff:
```python
import jax
import jax.numpy as jnp
from jax import lax
from jax.experimental import pallas as pl
from jax.experimental.pallas import tpu as pltpu
from jax.sharding import PartitionSpec as P

F32 = jnp.float32
BF16 = jnp.bfloat16
MESH = pl.DeviceIdType.MESH
ROWS = 36


def split(x):
    high = x.astype(BF16)
    return high, (x - high.astype(F32)).astype(BF16)


def dot(a, b, ca=1, cb=0):
    return lax.dot_general(a, b, (((ca,), (cb,)), ((), ())), preferred_element_type=F32)


def position():
    tm = lax.axis_index("tm")
    sp = lax.axis_index("space")
    return tm // 4, (tm // 2) % 2 * 2 + sp // 4, sp % 4, tm % 2


def device(z, x, y, c):
    return z * 4 + (x // 2) * 2 + c, (x % 2) * 4 + y


def partner(i, where):
    z, x, y, c = where
    a, b, e, d = i % 4, (i // 4) % 4, (i // 16) % 4, i // 64
    return device((z + a) % 4, (x + a + b) % 4, (y + a + b + e) % 4, (c + d + a) % 2)


def swap_lanes(pieces):
    lane = lax.broadcasted_iota(jnp.int32, (8, 128), 1)
    for bit in (1, 2, 4):
        low = (lane & bit) == 0
        moved = list(pieces)
        for p in range(8):
            if p & bit == 0:
                a, b = pieces[p], pieces[p | bit]
                moved[p] = jnp.where(low, a, pltpu.roll(b, bit, 1))
                moved[p | bit] = jnp.where(low, pltpu.roll(a, 128 - bit, 1), b)
        pieces = moved
    return pieces


def to_lines(chunks, lines):
    def body(i, carry):
        k, h = i // 6, i % 6
        for tau in range(2):
            for top in range(2):
                row = k * 12 + tau * 6 + h
                got = [
                    chunks[pl.ds((top * 8 + p) * 8 * ROWS + row, 8, stride=ROWS), :]
                    for p in range(8)
                ]
                base = pl.multiple_of(k * 384 + h * 64, 64)
                lanes = slice((top * 2 + tau) * 128, (top * 2 + tau + 1) * 128)
                for x8, piece in enumerate(swap_lanes(got)):
                    lines[pl.ds(base + x8 * 8, 8), lanes] = piece
        return carry

    lax.fori_loop(0, 18, body, 0)


def to_chunks(lines, chunks):
    def body(i, carry):
        k, h = i // 6, i % 6
        for tau in range(2):
            for top in range(2):
                row = k * 12 + tau * 6 + h
                base = pl.multiple_of(k * 384 + h * 64, 64)
                lanes = slice((top * 2 + tau) * 128, (top * 2 + tau + 1) * 128)
                got = [lines[pl.ds(base + x8 * 8, 8), lanes] for x8 in range(8)]
                for p, piece in enumerate(swap_lanes(got)):
                    chunks[pl.ds((top * 8 + p) * 8 * ROWS + row, 8, stride=ROWS), :] = piece
        return carry

    lax.fori_loop(0, 18, body, 0)


def forward_y(field, left, chunks):
    def body(i, carry):
        tau, h = i // 3, (i % 3) * 2
        v = field[pl.ds(pl.multiple_of(tau * 16, 16), 16), pl.ds(pl.multiple_of(h * 8, 16), 16), :]
        high, low = split(
            jnp.concatenate([v[:, 0:8].reshape(128, 384), v[:, 8:16].reshape(128, 384)], axis=0)
        )
        out = dot(left[...], jnp.concatenate([high, low, high], axis=1), 1, 1)
        for k in range(3):
            for j in range(2):
                chunks[pl.ds(k * 12 + tau * 6 + h + j, 128, stride=ROWS), :] = out[
                    k * 128 : (k + 1) * 128, j * 128 : (j + 1) * 128
                ]
        return carry

    lax.fori_loop(0, 6, body, 0)


def tripled(ref, values):
    high, low = split(values)
    width = values.shape[1]
    ref[:, 0:width] = high
    ref[:, width : 2 * width] = high
    ref[:, 2 * width : 3 * width] = low


def stacked(values):
    high, low = split(values)
    return jnp.concatenate([high, low, high], axis=0)


def forward_tx(lines, time_high, time_low, left_x, out):
    def body(k, carry):
        rows = pl.ds(pl.multiple_of(k * 384, 384), 384)
        high, low = split(lines[rows, :])
        mid = dot(high, time_high[...]) + dot(high, time_low[...]) + dot(low, time_high[...])
        out[rows, :] = dot(left_x[...], stacked(mid))
        return carry

    lax.fori_loop(0, 3, body, 0)


def send_all(where, copy_to):
    def body(i, carry):
        copy_to(*partner(i, where)).start()
        return carry

    lax.fori_loop(1, 128, body, 0)


def stencil(ext, reac, ycoef, xcoef, tcoef, mass, stiff, mixed, rest, image):
    def along_y(t, carry):
        for part in range(4):
            rows = slice(part * 16, part * 16 + 16)
            v = ext[t, rows, :]
            m = ycoef[3:4, :] * v
            s = ycoef[10:11, :] * v
            for off in (-3, -2, -1, 1, 2, 3):
                moved = pltpu.roll(v, (-off) % 384, 1)
                m = m + ycoef[3 + off : 4 + off, :] * moved
                s = s + ycoef[10 + off : 11 + off, :] * moved
            for c in range(3):
                mass[t, c, rows, :] = m[:, c * 128 : (c + 1) * 128]
                stiff[t, c, rows, :] = s[:, c * 128 : (c + 1) * 128]
        return carry

    lax.fori_loop(0, 38, along_y, 0)

    for i in range(6):
        first = i * 8
        ms = [xcoef[j, first : first + 8, :] for j in range(7)]
        ks = [xcoef[7 + j, first : first + 8, :] for j in range(7)]

        def along_x(t, carry):
            for c in range(3):
                m = [mass[t, c, 5 + j + first : 13 + j + first, :] for j in range(7)]
                s = [stiff[t, c, 5 + j + first : 13 + j + first, :] for j in range(7)]
                a = ms[0] * m[0]
                b = ks[0] * m[0] + ms[0] * s[0]
                for j in range(1, 7):
                    a = a + ms[j] * m[j]
                    b = b + (ks[j] * m[j] + ms[j] * s[j])
                mixed[t, c, first : first + 8, :] = a
                rest[t, c, first : first + 8, :] = b
            return carry

        lax.fori_loop(0, 38, along_x, 0)

    def along_t(t, total):
        kt = [tcoef[j * 32 + t] for j in range(7)]
        mt = [tcoef[(7 + j) * 32 + t] for j in range(7)]
        for c in range(3):
            lanes = slice(c * 128, c * 128 + 128)
            for i in range(6):
                rows = slice(i * 8, i * 8 + 8)
                own = ext[t + 3, 8 + i * 8 : 16 + i * 8, lanes]
                value = reac[t, rows, lanes] * own
                for j in range(7):
                    value = value + (
                        kt[j] * mixed[t + j, c, rows, :] + mt[j] * rest[t + j, c, rows, :]
                    )
                image[t, rows, lanes] = value
                total = total + own * value
        return total

    return lax.fori_loop(0, 32, along_t, jnp.zeros((8, 128), F32))


def whole(x):
    return jnp.sum(jnp.sum(x, axis=1, keepdims=True), axis=0, keepdims=True)


def main_kernel(
    r_h, d_h, reac_h, s_h, sp_h, tp_h, base_h, yc_h, xc_h, tcoef, seig,
    img_h, back_h, scal_o,
    rv, ext, reac, image, s_v, sp_v, tp_v, base_v, yc_v, xc_v,
    left_y, left_x, left_xi, time_high, time_low,
    send1, send2, send3, recv1, recv2, lines, hat_r, hat_i,
    mass, stiff, mixed, rest, red1s, red1, red2s, red2,
    local, halo_s, halo_r, out_sem, send_sem, recv_sem,
):
    where = position()
    tm = lax.axis_index("tm")
    sp = lax.axis_index("space")
    me = tm * 8 + sp
    loads = [
        pltpu.make_async_copy(src, dst, local.at[n])
        for n, (src, dst) in enumerate(
            [
                (d_h, ext.at[3:35, 8:56]), (s_h, s_v), (r_h, rv), (reac_h, reac),
                (sp_h, sp_v), (tp_h, tp_v), (base_h, base_v), (yc_h, yc_v), (xc_h, xc_v),
            ]
        )
    ]
    for load in loads:
        load.start()

    barrier = pltpu.get_barrier_semaphore()

    def greet(i, carry):
        pl.semaphore_signal(barrier, inc=1, device_id=partner(i, where), device_id_type=MESH)
        return carry

    lax.fori_loop(1, 128, greet, 0)
    loads[1].wait()
    tripled(left_y, s_v[...].T)
    loads[0].wait()
    pl.semaphore_wait(barrier, 127)

    halos = []
    for dt, src_t, dst_t in ((-1, slice(3, 6), slice(35, 38)), (0, slice(3, 35), slice(3, 35)), (1, slice(32, 35), slice(0, 3))):
        for dx, src_x, dst_x in ((-1, slice(8, 16), slice(56, 64)), (0, slice(8, 56), slice(8, 56)), (1, slice(48, 56), slice(0, 8))):
            if dt or dx:
                n = len(halos)
                halos.append(
                    pltpu.make_async_remote_copy(
                        src_ref=ext.at[src_t, src_x],
                        dst_ref=ext.at[dst_t, dst_x],
                        send_sem=halo_s.at[n],
                        recv_sem=halo_r.at[n],
                        device_id=((tm + 16 + dt) % 16, (sp + 8 + dx) % 8),
                        device_id_type=MESH,
                    )
                )
    for halo in halos:
        halo.start()

    def chunk(ref, d):
        return ref.at[pl.ds(d * ROWS, ROWS)]

    def exchange(n, src, dst):
        def copy_to(t, s):
            return pltpu.make_async_remote_copy(
                src_ref=chunk(src, t * 8 + s),
                dst_ref=chunk(dst, me),
                send_sem=send_sem.at[n],
                recv_sem=recv_sem.at[n],
                device_id=(t, s),
                device_id_type=MESH,
            )

        send_all(where, copy_to)

    def finish(n, src, dst, rows):
        return pltpu.make_async_remote_copy(
            src_ref=src.at[pl.ds(0, 127 * rows)],
            dst_ref=dst.at[pl.ds(0, 127 * rows)],
            send_sem=send_sem.at[n],
            recv_sem=recv_sem.at[n],
            device_id=(tm, sp),
            device_id_type=MESH,
        )

    def own_chunk(src, dst):
        dst[pl.ds(me * ROWS, ROWS), :] = src[pl.ds(me * ROWS, ROWS), :]

    loads[2].wait()
    forward_y(rv, left_y, send1)
    exchange(0, send1, recv1)
    own_chunk(send1, recv1)

    for load in loads[3:]:
        load.wait()
    for halo in halos:
        halo.wait()
    curve = stencil(ext, reac, yc_v, xc_v, tcoef, mass, stiff, mixed, rest, image)
    store_image = pltpu.make_async_copy(image, img_h, out_sem.at[0])
    store_image.start()
    forward_y(image, left_y, send2)
    exchange(1, send2, recv2)
    own_chunk(send2, recv2)

    tripled(left_x, sp_v[...].T)
    tripled(left_xi, sp_v[...])
    high, low = split(tp_v[...])
    time_high[...] = high
    time_low[...] = low

    finish(0, send1, recv1, ROWS).wait()
    to_lines(recv1, lines)
    forward_tx(lines, time_high, time_low, left_x, hat_r)

    def eigen(k):
        return base_v[...] + seig[k * 128 + me]

    def old_part(k, total):
        v = hat_r[pl.ds(pl.multiple_of(k * 384, 384), 384), :]
        return total + jnp.sum((v * (v / eigen(k))).reshape(48, 8, 512), axis=0)

    old = lax.fori_loop(0, 3, old_part, jnp.zeros((8, 512), F32))
    old = old[:, 0:128] + old[:, 128:256] + old[:, 256:384] + old[:, 384:512]

    def share(n, mine, every, rows):
        def copy_to(t, s):
            return pltpu.make_async_remote_copy(
                src_ref=mine,
                dst_ref=every.at[pl.ds(me * rows, rows)],
                send_sem=send_sem.at[n],
                recv_sem=recv_sem.at[n],
                device_id=(t, s),
                device_id_type=MESH,
            )

        send_all(where, copy_to)
        every[pl.ds(me * rows, rows), :] = mine[...]

    red1s[0:1, :] = jnp.sum(old, axis=0, keepdims=True)
    red1s[1:2, :] = jnp.sum(curve, axis=0, keepdims=True)
    share(3, red1s, red1, 2)

    finish(1, send2, recv2, ROWS).wait()
    to_lines(recv2, lines)
    forward_tx(lines, time_high, time_low, left_x, hat_i)

    finish(3, red1, red1, 2).wait()
    every = red1[...]
    even = lax.broadcasted_iota(jnp.int32, (256, 128), 0) % 2 == 0
    norm_old = whole(jnp.where(even, every, 0.0))
    step = norm_old / whole(jnp.where(even, 0.0, every))

    def inverse_part(k, total):
        rows = pl.ds(pl.multiple_of(k * 384, 384), 384)
        v = hat_r[rows, :] - step * hat_i[rows, :]
        g = v / eigen(k)
        high, low = split(dot(left_xi[...], stacked(g)))
        lines[rows, :] = (
            dot(high, time_high[...], 1, 1)
            + dot(high, time_low[...], 1, 1)
            + dot(low, time_high[...], 1, 1)
        )
        return total + jnp.sum((v * g).reshape(48, 8, 512), axis=0)

    new = lax.fori_loop(0, 3, inverse_part, jnp.zeros((8, 512), F32))
    to_chunks(lines, send3)
    exchange(2, send3, back_h)
    own = pltpu.make_async_copy(chunk(send3, me), chunk(back_h, me), out_sem.at[1])
    own.start()

    new = new[:, 0:128] + new[:, 128:256] + new[:, 256:384] + new[:, 384:512]
    red2s[...] = jnp.sum(new, axis=0, keepdims=True)
    share(4, red2s, red2, 1)
    finish(4, red2, red2, 1).wait()
    norm_new = whole(red2[...])
    row = lax.broadcasted_iota(jnp.int32, (8, 128), 0)
    scal_o[...] = jnp.where(row == 0, step, norm_new / norm_old)

    store_image.wait()
    own.wait()
    finish(2, send3, back_h, ROWS).wait()


def last_kernel(
    back_h, s_h, d_h, sol_h, r_h, img_h, scal,
    new_sol, new_res, new_dir,
    back, s_v, left, d_v, sol_v, r_v, img_v, ns_v, nr_v, nd_v, in_sem, out_sem,
):
    start = [pltpu.make_async_copy(s_h, s_v, in_sem.at[0]), pltpu.make_async_copy(back_h, back, in_sem.at[1])]
    halves = []
    for half in range(2):
        t = slice(half * 16, half * 16 + 16)
        halves.append(
            [
                pltpu.make_async_copy(src.at[t], dst.at[t], in_sem.at[2 + half * 4 + n])
                for n, (src, dst) in enumerate(((d_h, d_v), (sol_h, sol_v), (r_h, r_v), (img_h, img_v)))
            ]
        )
    for copy in start + halves[0] + halves[1]:
        copy.start()
    start[0].wait()
    tripled(left, s_v[...])
    start[1].wait()
    step = scal[0:1, 0:1]
    ratio = scal[1:2, 0:1]
    stores = []
    for tau in range(2):
        t = slice(tau * 16, tau * 16 + 16)
        for copy in halves[tau]:
            copy.wait()

        def body(i, carry):
            h = i * 2
            parts = []
            for j in range(2):
                parts.append(
                    jnp.concatenate(
                        [back[pl.ds(k * 12 + tau * 6 + h + j, 128, stride=ROWS), :] for k in range(3)], axis=0
                    )
                )
            out = dot(left[...], stacked(jnp.concatenate(parts, axis=1))).T
            for j in range(2):
                x = pl.ds(pl.multiple_of((h + j) * 8, 8), 8)
                d = d_v[t, x, :]
                nd_v[t, x, :] = out[j * 128 : (j + 1) * 128, :].reshape(16, 8, 384) + ratio.reshape(1, 1, 1) * d
                ns_v[t, x, :] = sol_v[t, x, :] + step.reshape(1, 1, 1) * d
                nr_v[t, x, :] = r_v[t, x, :] - step.reshape(1, 1, 1) * img_v[t, x, :]
            return carry

        lax.fori_loop(0, 3, body, 0)
        for n, (src, dst) in enumerate(((ns_v, new_sol), (nr_v, new_res), (nd_v, new_dir))):
            stores.append(pltpu.make_async_copy(src.at[t], dst.at[t], out_sem.at[tau * 3 + n]))
            stores[-1].start()
    for store in stores:
        store.wait()


def band_lines(table):
    n = table.shape[1]
    lines = []
    for off in range(-3, 4):
        size = abs(off)
        zeros = jnp.zeros((size,), F32)
        kept = table[size, : n - size]
        lines.append(jnp.concatenate([zeros, kept] if off < 0 else [kept, zeros]))
    return jnp.stack(lines)


ANY = pl.BlockSpec(memory_space=pl.ANY)
VMEM = pl.BlockSpec(memory_space=pltpu.VMEM)
SMEM = pl.BlockSpec(memory_space=pltpu.SMEM)


def per_device(solution, residual, direction, reaction, time_bands, space_bands, time_basis, space_basis, time_eigen, space_eigen):
    tm = lax.axis_index("tm")
    sp = lax.axis_index("space")
    space_lines = jnp.concatenate([band_lines(space_bands[1]), band_lines(space_bands[0])])
    time_lines = jnp.concatenate([band_lines(time_bands[0]), band_lines(time_bands[1])])
    x_lines = lax.dynamic_slice_in_dim(space_lines, sp * 48, 48, 1)
    t_lines = lax.dynamic_slice_in_dim(time_lines, tm * 32, 32, 1).reshape(-1)
    x_lines = jnp.broadcast_to(x_lines[:, :, None], (14, 48, 128))
    basis_x = space_basis.reshape(8, 6, 8, 384).transpose(1, 2, 0, 3).reshape(384, 384)
    basis_t = time_basis.reshape(2, 8, 2, 16, 512).transpose(0, 2, 3, 1, 4).reshape(512, 512)
    base = space_eigen[:, None] + time_eigen[None, :]
    block = (32, 48, 384)
    chunks = (128 * ROWS, 128)
    v = pltpu.VMEM
    dma = pltpu.SemaphoreType.DMA
    image, back, scal = pl.pallas_call(
        main_kernel,
        out_shape=(
            jax.ShapeDtypeStruct(block, F32),
            jax.ShapeDtypeStruct(chunks, F32),
            jax.ShapeDtypeStruct((8, 128), F32),
        ),
        in_specs=[ANY] * 9 + [SMEM] * 2,
        out_specs=(ANY, ANY, VMEM),
        scratch_shapes=[
            v(block, F32), v((38, 64, 384), F32), v(block, F32), v(block, F32),
            v((384, 384), F32), v((384, 384), F32), v((512, 512), F32), v((384, 512), F32),
            v((14, 384), F32), v((14, 48, 128), F32),
            v((384, 1152), BF16), v((384, 1152), BF16), v((384, 1152), BF16),
            v((512, 512), BF16), v((512, 512), BF16),
            v(chunks, F32), v(chunks, F32), v(chunks, F32), v(chunks, F32), v(chunks, F32),
            v((1152, 512), F32), v((1152, 512), F32), v((1152, 512), F32),
            v((38, 3, 64, 128), F32), v((38, 3, 64, 128), F32),
            v((38, 3, 48, 128), F32), v((38, 3, 48, 128), F32),
            v((2, 128), F32), v((256, 128), F32), v((1, 128), F32), v((128, 128), F32),
            dma((9,)), dma((8,)), dma((8,)), dma((2,)), dma((5,)), dma((5,)),
        ],
        compiler_params=pltpu.CompilerParams(
            collective_id=0, has_side_effects=True, vmem_limit_bytes=62 * 2**20
        ),
    )(residual, direction, reaction, space_basis, basis_x, basis_t, base, space_lines, x_lines, t_lines, space_eigen)
    return pl.pallas_call(
        last_kernel,
        out_shape=(jax.ShapeDtypeStruct(block, F32),) * 3,
        in_specs=[ANY] * 6 + [VMEM],
        out_specs=(ANY,) * 3,
        scratch_shapes=[
            v(chunks, F32), v((384, 384), F32), v((384, 1152), BF16),
            *[v(block, F32) for _ in range(7)],
            dma((10,)), dma((6,)),
        ],
        compiler_params=pltpu.CompilerParams(vmem_limit_bytes=48 * 2**20),
    )(back, space_basis, direction, solution, residual, image, scal)


def solution(mesh):
    field = P("tm", "space", None)
    return jax.shard_map(
        per_device,
        mesh=mesh,
        in_specs=(field,) * 4 + (P(),) * 6,
        out_specs=(field,) * 3,
        check_vma=False,
    )
```

time: 537 us -> 168 us (0.31); the launches traced: 526 us -> 167 us
  Pallas kernels: 0 us -> 151 us
  blocking collectives: 133 us -> 0 us
  local copies, waits for them, and re-layouts: 122 us -> 13 us
  other arithmetic: 100 us -> 1.92 us
  waiting for transfers between devices: 83.8 us -> 0 us
  matrix products: 52 us -> 0 us
  starting transfers between devices: 30.4 us -> 0 us
    pallas_call x0 -> x2, Pallas kernels: none -> 151 us  [the longest x1 144 us: per_device(): pl.pallas_call(main_kernel, out_shape=(jax.ShapeDtypeStruct(block, F32),...]
    all_to_all x3 -> x0, blocking collectives: 100 us -> none  [the longest x1 57.9 us: forward_fields(): lax.all_to_all(along_y, SPACE, split_axis=3, concat_axis=2, tiled=True)]
    all_to_all x2 -> x0, waiting for transfers between devices: 76.7 us -> none  [the longest x1 56.2 us: forward_fields(): lax.all_to_all(along_x, TM, split_axis=3, concat_axis=1, tiled=True)]
    dot_general x6 -> x0, matrix products: 52 us -> none  [the longest x1 11.8 us: forward_fields(): jnp.einsum('ctjy,jb->ctby', spread, space_basis, precision=highest)]
    add x4 -> x1, other arithmetic: 48.4 us -> 1.7 us  [per_device(): base = space_eigen[:, None] + time_eigen[None, :]]
    unnamed x30 -> x12, local copies, waits for them, and re-layouts: 48.1 us -> 4.02 us
    all_to_all x7 -> x0, local copies, waits for them, and re-layouts: 40.4 us -> none  [the longest x3 27.9 us: forward_fields(): lax.all_to_all(along_y, SPACE, split_axis=3, concat_axis=2, tiled=True)]
    psum x5 -> x0, blocking collectives: 33 us -> none  [over_axes(): shard = lax.psum(shard, axis)]
  transfers between devices with their start and end apart: 6 -> 0, of which waited for: 5 -> 0; matrix products, arithmetic and copies ran while one was open for 2% -> 0% of each run, Pallas kernels for 0% -> 0%
where the time goes in v1:
time: 168 us; the launch traced here: 167 us
  Pallas kernels  151 us (90%)
  local copies, waits for them, and re-layouts  13 us (8%)
  other arithmetic  1.92 us (1%)
    pallas_call x1, Pallas kernels, per_device(): pl.pallas_call(main_kernel, out_shape=(jax.ShapeDtypeStruct(block, F32),...  144 us
    pallas_call x1, Pallas kernels, per_device(): pl.pallas_call(last_kernel, out_shape=(jax.ShapeDtypeStruct(block, F32),)...  7.78 us
    unnamed x12, local copies, waits for them, and re-layouts  4.02 us

profile of v1, /device:TPU:1, one launch (start us, length us, event | category | flops | bytes accessed | tf_op | source)
XLA Modules:
  0.0 167.1 jit_solution(6214975440852946017)
XLA Ops:
  0.6 0.0 copy-start.4
  0.6 0.8 slice_bitcast_fusion.6
  1.4 0.7 slice_bitcast_fusion.4
  2.2 0.7 slice_bitcast_fusion.2
  2.9 0.1 pad_maximum_fusion.2
  3.0 0.1 pad_maximum_fusion.3
  3.1 0.1 fusion.5
  3.2 0.1 fusion.4
  3.3 0.1 fusion.7
  3.4 0.1 fusion.6
  3.4 0.1 concatenate.90.yc_h
  3.5 0.0 copy-start.5
  3.5 0.1 constant_dynamic-slice_fusion.1
  3.6 0.7 slice_bitcast_fusion
  4.4 0.1 fusion.2
  4.4 0.1 pad_maximum_fusion.6
  4.5 0.1 fusion
  4.6 0.1 concatenate.103
  4.7 0.1 constant_dynamic-slice_fusion
  4.7 0.6 reshape.32.tcoef
  5.4 0.9 broadcast_in_dim.2.xc_h
  6.3 2.1 %copy.13 = f32[8,6,8,384]{3,0,2,1:T(8,128)} copy(f32[8,6,8,384]{3,2,1,0:T(8,128)} %bitcast.42) | data formatting | bytes 1179648 | tf_op jit(solution)/shard_map/reshape | solution.py:457
  8.4 1.7 %broadcast_add_fusion.base_h = f32[384,512]{1,0:T(8,128)} fusion(f32[512]{0:T(512)} %param.18, f32[384]{0:T(512)} %seig.1), kind=kLoop, calls=%fused_computation | loop fusion | flops 196608 | bytes 790016 | tf_op jit(solution)/shard_map/add | solution.py:459
  10.1 0.0 copy-done.4
  10.1 1.6 copy.14
  11.6 0.0 copy-done.5
  11.6 0.0 copy-start.1
  11.6 143.6 %shard_map.121 = (f32[32,48,384]{2,1,0:T(8,128)}, f32[4608,128]{1,0:T(8,128)}, f32[8,128]{1,0:T(8,128)}) custom-call(f32[32,48,384]{2,1,0:T(8,128)} %r_h.3, f32[32,48,384]{2,1,0:T(8,128)} %d_h.3, f32[32,48,384]{2,1,0:T(8,128)} %reac_h.1, f32[384,384]{1,0:T(8,128)} %s_h.3, f32[384,384]{1,0:T(8,128)} %bitcast.44, f32[512,512]{1,0:T(8,128)} %bitcast.43, ...), custom_call_target="tpu_custom_call" | custom-call | tf_op jit(solution)/shard_map/pallas_call | solution.py:464
  155.2 0.0 copy-done.1
  155.3 0.0 copy-start
  155.3 1.7 copy-done
  156.9 0.0 copy-start.2
  156.9 1.7 copy-done.2
  158.6 0.0 copy-start.3
  158.6 0.7 copy-done.3
  159.3 7.8 %shard_map.122 = (f32[32,48,384]{2,1,0:T(8,128)}, f32[32,48,384]{2,1,0:T(8,128)}, f32[32,48,384]{2,1,0:T(8,128)}) custom-call(f32[4608,128]{1,0:T(8,128)S(1)} %copy-done.2, f32[384,384]{1,0:T(8,128)S(1)} %copy-done.1, f32[32,48,384]{2,1,0:T(8,128)S(1)} %copy-done, f32[32,48,384]{2,1,0:T(8,128)} %sol_h.1, f32[32,48,384]{2,1,0:T(8,128)} %r_h.3, ...), custom_call_target="tpu_custom_call" | custom-call | tf_op jit(solution)/shard_map/pallas_call | solution.py:490
  (21 shorter events, 0.1 us)
Async XLA Ops:
  0.6 9.4 %copy-start.4 = (f32[512,512]{1,0:T(8,128)S(1)}, f32[512,512]{1,0:T(8,128)}, u32[]{:S(2)}) copy-start(f32[512,512]{1,0:T(8,128)} %param.16) | copy-start | bytes 3145732
  3.5 8.1 %copy-start.5 = (f32[14,384]{1,0:T(8,128)}, f32[14,384]{1,0:T(8,128)S(1)}, u32[]{:S(2)}) copy-start(f32[14,384]{1,0:T(8,128)S(1)} %concatenate.90.yc_h) | copy-start | bytes 64516
  11.6 143.6 %copy-start.1 = (f32[384,384]{1,0:T(8,128)S(1)}, f32[384,384]{1,0:T(8,128)}, u32[]{:S(2)}) copy-start(f32[384,384]{1,0:T(8,128)} %s_h.3) | copy-start | bytes 1769476
  155.3 1.7 copy-start
  156.9 1.7 copy-start.2
  158.6 0.7 copy-start.3

commit v2 on v1

--- a/solution.py
+++ b/solution.py
@@ -50,9 +50,8 @@
     return pieces
 
 
-def to_lines(chunks, lines):
-    def body(i, carry):
-        k, h = i // 6, i % 6
+def to_lines(chunks, k, lines):
+    def body(h, carry):
         for tau in range(2):
             for top in range(2):
                 row = k * 12 + tau * 6 + h
@@ -60,42 +59,50 @@
                     chunks[pl.ds((top * 8 + p) * 8 * ROWS + row, 8, stride=ROWS), :]
                     for p in range(8)
                 ]
-                base = pl.multiple_of(k * 384 + h * 64, 64)
+                base = pl.multiple_of(h * 64, 64)
                 lanes = slice((top * 2 + tau) * 128, (top * 2 + tau + 1) * 128)
                 for x8, piece in enumerate(swap_lanes(got)):
                     lines[pl.ds(base + x8 * 8, 8), lanes] = piece
         return carry
 
-    lax.fori_loop(0, 18, body, 0)
-
-
-def to_chunks(lines, chunks):
-    def body(i, carry):
-        k, h = i // 6, i % 6
+    lax.fori_loop(0, 6, body, 0)
+
+
+def to_chunks(lines, k, chunks):
+    def body(h, carry):
         for tau in range(2):
             for top in range(2):
                 row = k * 12 + tau * 6 + h
-                base = pl.multiple_of(k * 384 + h * 64, 64)
+                base = pl.multiple_of(h * 64, 64)
                 lanes = slice((top * 2 + tau) * 128, (top * 2 + tau + 1) * 128)
                 got = [lines[pl.ds(base + x8 * 8, 8), lanes] for x8 in range(8)]
                 for p, piece in enumerate(swap_lanes(got)):
                     chunks[pl.ds((top * 8 + p) * 8 * ROWS + row, 8, stride=ROWS), :] = piece
         return carry
 
-    lax.fori_loop(0, 18, body, 0)
-
-
-def forward_y(field, left, chunks):
+    lax.fori_loop(0, 6, body, 0)
+
+
+def pack_rows(field, packed):
     def body(i, carry):
-        tau, h = i // 3, (i % 3) * 2
-        v = field[pl.ds(pl.multiple_of(tau * 16, 16), 16), pl.ds(pl.multiple_of(h * 8, 16), 16), :]
-        high, low = split(
-            jnp.concatenate([v[:, 0:8].reshape(128, 384), v[:, 8:16].reshape(128, 384)], axis=0)
-        )
-        out = dot(left[...], jnp.concatenate([high, low, high], axis=1), 1, 1)
+        tau, h = i // 6, i % 6
+        v = field[pl.ds(pl.multiple_of(tau * 16, 16), 16), pl.ds(pl.multiple_of(h * 8, 8), 8), :]
+        high, low = split(v.reshape(128, 384))
+        rows = pl.ds(pl.multiple_of(i * 128, 128), 128)
+        packed[rows, 0:384] = high
+        packed[rows, 384:768] = low
+        packed[rows, 768:1152] = high
+        return carry
+
+    lax.fori_loop(0, 12, body, 0)
+
+
+def forward_y(packed, left, chunks):
+    def body(i, carry):
+        out = dot(left[...], packed[pl.ds(pl.multiple_of(i * 256, 256), 256), :], 1, 1)
         for k in range(3):
             for j in range(2):
-                chunks[pl.ds(k * 12 + tau * 6 + h + j, 128, stride=ROWS), :] = out[
+                chunks[pl.ds(k * 12 + i * 2 + j, 128, stride=ROWS), :] = out[
                     k * 128 : (k + 1) * 128, j * 128 : (j + 1) * 128
                 ]
         return carry
@@ -116,15 +123,10 @@
     return jnp.concatenate([high, low, high], axis=0)
 
 
-def forward_tx(lines, time_high, time_low, left_x, out):
-    def body(k, carry):
-        rows = pl.ds(pl.multiple_of(k * 384, 384), 384)
-        high, low = split(lines[rows, :])
-        mid = dot(high, time_high[...]) + dot(high, time_low[...]) + dot(low, time_high[...])
-        out[rows, :] = dot(left_x[...], stacked(mid))
-        return carry
-
-    lax.fori_loop(0, 3, body, 0)
+def forward_tx(lines, time_high, time_low, left_x):
+    high, low = split(lines[...])
+    mid = dot(high, time_high[...]) + dot(high, time_low[...]) + dot(low, time_high[...])
+    return dot(left_x[...], stacked(mid))
 
 
 def send_all(where, copy_to):
@@ -135,10 +137,17 @@
     lax.fori_loop(1, 128, body, 0)
 
 
-def stencil(ext, reac, ycoef, xcoef, tcoef, mass, stiff, mixed, rest, image):
+def stencil(ext, reac, ycoef, xcoef, tbands, first_t, tcoef, mass, stiff, mixed, rest, image):
+    def time_weight(matrix, off, t):
+        size = abs(off)
+        if off <= 0:
+            value = tbands[matrix, size, jnp.maximum(t - size, 0)]
+            return jnp.where(t >= size, value, 0.0)
+        return jnp.where(t + size < 512, tbands[matrix, size, t], 0.0)
+
     def along_y(t, carry):
-        for part in range(4):
-            rows = slice(part * 16, part * 16 + 16)
+        for part in range(2):
+            rows = slice(part * 32, part * 32 + 32)
             v = ext[t, rows, :]
             m = ycoef[3:4, :] * v
             s = ycoef[10:11, :] * v
@@ -173,52 +182,73 @@
 
         lax.fori_loop(0, 38, along_x, 0)
 
-    def along_t(t, total):
-        kt = [tcoef[j * 32 + t] for j in range(7)]
-        mt = [tcoef[(7 + j) * 32 + t] for j in range(7)]
+    def weights(t, carry):
+        for j in range(7):
+            tcoef[t * 14 + j] = time_weight(0, j - 3, first_t + t)
+            tcoef[t * 14 + 7 + j] = time_weight(1, j - 3, first_t + t)
+        return carry
+
+    lax.fori_loop(0, 32, weights, 0)
+
+    def along_t(pair, total):
+        t = pair * 2
+        kt = [[tcoef[(t + n) * 14 + j] for j in range(7)] for n in range(2)]
+        mt = [[tcoef[(t + n) * 14 + 7 + j] for j in range(7)] for n in range(2)]
         for c in range(3):
             lanes = slice(c * 128, c * 128 + 128)
             for i in range(6):
                 rows = slice(i * 8, i * 8 + 8)
-                own = ext[t + 3, 8 + i * 8 : 16 + i * 8, lanes]
-                value = reac[t, rows, lanes] * own
-                for j in range(7):
-                    value = value + (
-                        kt[j] * mixed[t + j, c, rows, :] + mt[j] * rest[t + j, c, rows, :]
-                    )
-                image[t, rows, lanes] = value
-                total = total + own * value
+                own = [ext[t + 3 + n, 8 + i * 8 : 16 + i * 8, lanes] for n in range(2)]
+                value = [reac[t + n, rows, lanes] * own[n] for n in range(2)]
+                for j in range(8):
+                    a = mixed[t + j, c, rows, :]
+                    b = rest[t + j, c, rows, :]
+                    for n in range(2):
+                        if 0 <= j - n < 7:
+                            value[n] = value[n] + (kt[n][j - n] * a + mt[n][j - n] * b)
+                for n in range(2):
+                    image[t + n, rows, lanes] = value[n]
+                    total = total + own[n] * value[n]
         return total
 
-    return lax.fori_loop(0, 32, along_t, jnp.zeros((8, 128), F32))
+    return lax.fori_loop(0, 16, along_t, jnp.zeros((8, 128), F32))
 
 
 def whole(x):
     return jnp.sum(jnp.sum(x, axis=1, keepdims=True), axis=0, keepdims=True)
 
 
+def band_lines(table):
+    lane = lax.broadcasted_iota(jnp.int32, (1, 384), 1)
+    lines = []
+    for off in range(-3, 4):
+        size = abs(off)
+        line = table[size : size + 1, :]
+        if off < 0:
+            line = jnp.where(lane >= size, pltpu.roll(line, size, 1), 0.0)
+        elif off > 0:
+            line = jnp.where(lane < 384 - size, line, 0.0)
+        lines.append(line)
+    return lines
+
+
 def main_kernel(
-    r_h, d_h, reac_h, s_h, sp_h, tp_h, base_h, yc_h, xc_h, tcoef, seig,
+    r_h, d_h, reac_h, s_h, t_h, sb_h, te_h, se_h, tbands, seig,
     img_h, back_h, scal_o,
-    rv, ext, reac, image, s_v, sp_v, tp_v, base_v, yc_v, xc_v,
-    left_y, left_x, left_xi, time_high, time_low,
-    send1, send2, send3, recv1, recv2, lines, hat_r, hat_i,
+    rv, ext, reac, image, s_v, s3, t4, sb_v, te_v, se_v, base_v, yc_v, xt_v, xc_v, sp_v,
+    left_y, left_x, left_xi, time_high, time_low, packed,
+    send1, send2, recv1, recv2, lines, hat_r,
     mass, stiff, mixed, rest, red1s, red1, red2s, red2,
-    local, halo_s, halo_r, out_sem, send_sem, recv_sem,
+    tcoef, local, halo_s, halo_r, out_sem, send_sem, recv_sem,
 ):
     where = position()
     tm = lax.axis_index("tm")
     sp = lax.axis_index("space")
     me = tm * 8 + sp
-    loads = [
-        pltpu.make_async_copy(src, dst, local.at[n])
-        for n, (src, dst) in enumerate(
-            [
-                (d_h, ext.at[3:35, 8:56]), (s_h, s_v), (r_h, rv), (reac_h, reac),
-                (sp_h, sp_v), (tp_h, tp_v), (base_h, base_v), (yc_h, yc_v), (xc_h, xc_v),
-            ]
-        )
-    ]
+    pairs = [(d_h, ext.at[3:35, 8:56]), (s_h, s_v), (r_h, rv), (sb_h, sb_v), (reac_h, reac), (te_h, te_v), (se_h, se_v)]
+    pairs += [(s_h.at[:, c * 128 : c * 128 + 128], s3.at[c]) for c in range(3)]
+    pairs += [(t_h.at[:, c * 128 : c * 128 + 128], t4.at[c]) for c in range(4)]
+    loads = [pltpu.make_async_copy(src, dst, local.at[n]) for n, (src, dst) in enumerate(pairs)]
     for load in loads:
         load.start()
 
@@ -231,12 +261,15 @@
     lax.fori_loop(1, 128, greet, 0)
     loads[1].wait()
     tripled(left_y, s_v[...].T)
+    loads[2].wait()
+    pack_rows(rv, packed)
+    forward_y(packed, left_y, send1)
     loads[0].wait()
     pl.semaphore_wait(barrier, 127)
 
     halos = []
     for dt, src_t, dst_t in ((-1, slice(3, 6), slice(35, 38)), (0, slice(3, 35), slice(3, 35)), (1, slice(32, 35), slice(0, 3))):
-        for dx, src_x, dst_x in ((-1, slice(8, 16), slice(56, 64)), (0, slice(8, 56), slice(8, 56)), (1, slice(48, 56), slice(0, 8))):
+        for dx, src_x, dst_x in ((-1, slice(8, 11), slice(56, 59)), (0, slice(8, 56), slice(8, 56)), (1, slice(53, 56), slice(5, 8))):
             if dt or dx:
                 n = len(halos)
                 halos.append(
@@ -252,16 +285,16 @@
     for halo in halos:
         halo.start()
 
-    def chunk(ref, d):
-        return ref.at[pl.ds(d * ROWS, ROWS)]
-
-    def exchange(n, src, dst):
+    def piece(ref, d, k):
+        return ref.at[pl.ds(d * ROWS + k * 12, 12)]
+
+    def exchange(n, src, dst, k):
         def copy_to(t, s):
             return pltpu.make_async_remote_copy(
-                src_ref=chunk(src, t * 8 + s),
-                dst_ref=chunk(dst, me),
-                send_sem=send_sem.at[n],
-                recv_sem=recv_sem.at[n],
+                src_ref=piece(src, t * 8 + s, k),
+                dst_ref=piece(dst, me, k),
+                send_sem=send_sem.at[n * 3 + k],
+                recv_sem=recv_sem.at[n * 3 + k],
                 device_id=(t, s),
                 device_id_type=MESH,
             )
@@ -281,37 +314,59 @@
     def own_chunk(src, dst):
         dst[pl.ds(me * ROWS, ROWS), :] = src[pl.ds(me * ROWS, ROWS), :]
 
-    loads[2].wait()
-    forward_y(rv, left_y, send1)
-    exchange(0, send1, recv1)
+    for k in range(3):
+        exchange(0, send1, recv1, k)
     own_chunk(send1, recv1)
 
-    for load in loads[3:]:
+    loads[3].wait()
+    table = jnp.concatenate(band_lines(sb_v[1]) + band_lines(sb_v[0]) + [jnp.zeros((2, 384), F32)], axis=0)
+    yc_v[...] = table
+    xt_v[...] = table.T
+    near = xt_v[pl.ds(pl.multiple_of(sp * 48, 16), 48), :]
+    for j in range(14):
+        xc_v[j] = jnp.broadcast_to(near[:, j : j + 1], (48, 128))
+    for load in loads[4:]:
         load.wait()
     for halo in halos:
         halo.wait()
-    curve = stencil(ext, reac, yc_v, xc_v, tcoef, mass, stiff, mixed, rest, image)
+    curve = stencil(ext, reac, yc_v, xc_v, tbands, tm * 32, tcoef, mass, stiff, mixed, rest, image)
     store_image = pltpu.make_async_copy(image, img_h, out_sem.at[0])
     store_image.start()
-    forward_y(image, left_y, send2)
-    exchange(1, send2, recv2)
+    pack_rows(image, packed)
+
+    forward_y(packed, left_y, send2)
+    exchange(1, send2, recv2, 0)
+    exchange(1, send2, recv2, 1)
     own_chunk(send2, recv2)
 
+    for h in range(48):
+        for c in range(3):
+            sp_v[h * 8 : h * 8 + 8, c * 128 : c * 128 + 128] = s3[c, pl.ds(h, 8, stride=48), :]
     tripled(left_x, sp_v[...].T)
     tripled(left_xi, sp_v[...])
-    high, low = split(tp_v[...])
-    time_high[...] = high
-    time_low[...] = low
-
-    finish(0, send1, recv1, ROWS).wait()
-    to_lines(recv1, lines)
-    forward_tx(lines, time_high, time_low, left_x, hat_r)
+
+    def time_rows(i, carry):
+        start = (i // 16) * 256 + (i // 8) % 2 * 16 + i % 8 * 2
+        rows = pl.ds(pl.multiple_of(i * 16, 16), 16)
+        for c in range(4):
+            got = jnp.concatenate([t4[c, pl.ds(start + j, 8, stride=32), :] for j in range(2)], axis=0)
+            high, low = split(got)
+            time_high[rows, c * 128 : c * 128 + 128] = high
+            time_low[rows, c * 128 : c * 128 + 128] = low
+        return carry
+
+    lax.fori_loop(0, 32, time_rows, 0)
+    column = jnp.broadcast_to(se_v[...], (8, 384)).T
+    base_v[...] = column[:, 0:1] + te_v[...]
 
     def eigen(k):
         return base_v[...] + seig[k * 128 + me]
 
     def old_part(k, total):
-        v = hat_r[pl.ds(pl.multiple_of(k * 384, 384), 384), :]
+        finish(k, send1, recv1, 12).wait()
+        to_lines(recv1, k, lines)
+        v = forward_tx(lines, time_high, time_low, left_x)
+        hat_r[pl.ds(pl.multiple_of(k * 384, 384), 384), :] = v
         return total + jnp.sum((v * (v / eigen(k))).reshape(48, 8, 512), axis=0)
 
     old = lax.fori_loop(0, 3, old_part, jnp.zeros((8, 512), F32))
@@ -333,47 +388,49 @@
 
     red1s[0:1, :] = jnp.sum(old, axis=0, keepdims=True)
     red1s[1:2, :] = jnp.sum(curve, axis=0, keepdims=True)
-    share(3, red1s, red1, 2)
-
-    finish(1, send2, recv2, ROWS).wait()
-    to_lines(recv2, lines)
-    forward_tx(lines, time_high, time_low, left_x, hat_i)
-
-    finish(3, red1, red1, 2).wait()
+    share(9, red1s, red1, 2)
+    exchange(1, send2, recv2, 2)
+
+    finish(9, red1, red1, 2).wait()
     every = red1[...]
     even = lax.broadcasted_iota(jnp.int32, (256, 128), 0) % 2 == 0
     norm_old = whole(jnp.where(even, every, 0.0))
     step = norm_old / whole(jnp.where(even, 0.0, every))
 
     def inverse_part(k, total):
+        finish(3 + k, send2, recv2, 12).wait()
+        to_lines(recv2, k, lines)
         rows = pl.ds(pl.multiple_of(k * 384, 384), 384)
-        v = hat_r[rows, :] - step * hat_i[rows, :]
+        v = hat_r[rows, :] - step * forward_tx(lines, time_high, time_low, left_x)
         g = v / eigen(k)
         high, low = split(dot(left_xi[...], stacked(g)))
-        lines[rows, :] = (
+        lines[...] = (
             dot(high, time_high[...], 1, 1)
             + dot(high, time_low[...], 1, 1)
             + dot(low, time_high[...], 1, 1)
         )
+        to_chunks(lines, k, send1)
+        exchange(2, send1, back_h, k)
         return total + jnp.sum((v * g).reshape(48, 8, 512), axis=0)
 
     new = lax.fori_loop(0, 3, inverse_part, jnp.zeros((8, 512), F32))
-    to_chunks(lines, send3)
-    exchange(2, send3, back_h)
-    own = pltpu.make_async_copy(chunk(send3, me), chunk(back_h, me), out_sem.at[1])
+    own = pltpu.make_async_copy(
+        send1.at[pl.ds(me * ROWS, ROWS)], back_h.at[pl.ds(me * ROWS, ROWS)], out_sem.at[1]
+    )
     own.start()
 
     new = new[:, 0:128] + new[:, 128:256] + new[:, 256:384] + new[:, 384:512]
     red2s[...] = jnp.sum(new, axis=0, keepdims=True)
-    share(4, red2s, red2, 1)
-    finish(4, red2, red2, 1).wait()
+    share(10, red2s, red2, 1)
+    finish(10, red2, red2, 1).wait()
     norm_new = whole(red2[...])
     row = lax.broadcasted_iota(jnp.int32, (8, 128), 0)
     scal_o[...] = jnp.where(row == 0, step, norm_new / norm_old)
 
     store_image.wait()
     own.wait()
-    finish(2, send3, back_h, ROWS).wait()
+    for k in range(3):
+        finish(6 + k, send1, back_h, 12).wait()
 
 
 def last_kernel(
@@ -430,33 +487,12 @@
         store.wait()
 
 
-def band_lines(table):
-    n = table.shape[1]
-    lines = []
-    for off in range(-3, 4):
-        size = abs(off)
-        zeros = jnp.zeros((size,), F32)
-        kept = table[size, : n - size]
-        lines.append(jnp.concatenate([zeros, kept] if off < 0 else [kept, zeros]))
-    return jnp.stack(lines)
-
-
-ANY = pl.BlockSpec(memory_space=pl.ANY)
 VMEM = pl.BlockSpec(memory_space=pltpu.VMEM)
+HBM = pl.BlockSpec(memory_space=pltpu.HBM)
 SMEM = pl.BlockSpec(memory_space=pltpu.SMEM)
 
 
 def per_device(solution, residual, direction, reaction, time_bands, space_bands, time_basis, space_basis, time_eigen, space_eigen):
-    tm = lax.axis_index("tm")
-    sp = lax.axis_index("space")
-    space_lines = jnp.concatenate([band_lines(space_bands[1]), band_lines(space_bands[0])])
-    time_lines = jnp.concatenate([band_lines(time_bands[0]), band_lines(time_bands[1])])
-    x_lines = lax.dynamic_slice_in_dim(space_lines, sp * 48, 48, 1)
-    t_lines = lax.dynamic_slice_in_dim(time_lines, tm * 32, 32, 1).reshape(-1)
-    x_lines = jnp.broadcast_to(x_lines[:, :, None], (14, 48, 128))
-    basis_x = space_basis.reshape(8, 6, 8, 384).transpose(1, 2, 0, 3).reshape(384, 384)
-    basis_t = time_basis.reshape(2, 8, 2, 16, 512).transpose(0, 2, 3, 1, 4).reshape(512, 512)
-    base = space_eigen[:, None] + time_eigen[None, :]
     block = (32, 48, 384)
     chunks = (128 * ROWS, 128)
     v = pltpu.VMEM
@@ -468,36 +504,40 @@
             jax.ShapeDtypeStruct(chunks, F32),
             jax.ShapeDtypeStruct((8, 128), F32),
         ),
-        in_specs=[ANY] * 9 + [SMEM] * 2,
-        out_specs=(ANY, ANY, VMEM),
+        in_specs=[HBM] * 8 + [SMEM] * 2,
+        out_specs=(HBM, HBM, VMEM),
         scratch_shapes=[
             v(block, F32), v((38, 64, 384), F32), v(block, F32), v(block, F32),
-            v((384, 384), F32), v((384, 384), F32), v((512, 512), F32), v((384, 512), F32),
-            v((14, 384), F32), v((14, 48, 128), F32),
+            v((384, 384), F32), v((3, 384, 128), F32), v((4, 512, 128), F32), v((2, 4, 384), F32),
+            v((1, 512), F32), v((1, 384), F32), v((384, 512), F32),
+            v((16, 384), F32), v((384, 16), F32), v((14, 48, 128), F32), v((384, 384), F32),
             v((384, 1152), BF16), v((384, 1152), BF16), v((384, 1152), BF16),
-            v((512, 512), BF16), v((512, 512), BF16),
-            v(chunks, F32), v(chunks, F32), v(chunks, F32), v(chunks, F32), v(chunks, F32),
-            v((1152, 512), F32), v((1152, 512), F32), v((1152, 512), F32),
+            v((512, 512), BF16), v((512, 512), BF16), v((1536, 1152), BF16),
+            v(chunks, F32), v(chunks, F32), v(chunks, F32), v(chunks, F32),
+            v((384, 512), F32), v((1152, 512), F32),
             v((38, 3, 64, 128), F32), v((38, 3, 64, 128), F32),
             v((38, 3, 48, 128), F32), v((38, 3, 48, 128), F32),
             v((2, 128), F32), v((256, 128), F32), v((1, 128), F32), v((128, 128), F32),
-            dma((9,)), dma((8,)), dma((8,)), dma((2,)), dma((5,)), dma((5,)),
+            pltpu.SMEM((448,), F32), dma((14,)), dma((8,)), dma((8,)), dma((2,)), dma((11,)), dma((11,)),
         ],
         compiler_params=pltpu.CompilerParams(
             collective_id=0, has_side_effects=True, vmem_limit_bytes=62 * 2**20
         ),
-    )(residual, direction, reaction, space_basis, basis_x, basis_t, base, space_lines, x_lines, t_lines, space_eigen)
+    )(
+        residual, direction, reaction, space_basis, time_basis, space_bands,
+        time_eigen.reshape(1, -1), space_eigen.reshape(1, -1), time_bands, space_eigen,
+    )
     return pl.pallas_call(
         last_kernel,
         out_shape=(jax.ShapeDtypeStruct(block, F32),) * 3,
-        in_specs=[ANY] * 6 + [VMEM],
-        out_specs=(ANY,) * 3,
+        in_specs=[HBM] * 6 + [VMEM],
+        out_specs=(HBM,) * 3,
         scratch_shapes=[
             v(chunks, F32), v((384, 384), F32), v((384, 1152), BF16),
             *[v(block, F32) for _ in range(7)],
             dma((10,)), dma((6,)),
         ],
-        compiler_params=pltpu.CompilerParams(vmem_limit_bytes=48 * 2**20),
+        compiler_params=pltpu.CompilerParams(vmem_limit_bytes=62 * 2**20),
     )(back, space_basis, direction, solution, residual, image, scal)
 
 

time: 168 us -> 149 us (0.89)
  local copies, waits for them, and re-layouts: 13 us -> 1.25 us
  Pallas kernels: 151 us -> 146 us
  other arithmetic: 1.92 us -> 0 us
    pallas_call x1, Pallas kernels: 144 us -> 137 us  [per_device(): pl.pallas_call(main_kernel, out_shape=(jax.ShapeDtypeStruct(block, F32),...]
    unnamed x12 -> x0, local copies, waits for them, and re-layouts: 4.02 us -> none
    reshape x3 -> x1, local copies, waits for them, and re-layouts: 4.29 us -> 1.25 us  [per_device(): space_eigen.reshape(1, -1)]
    add x1 -> x0, other arithmetic: 1.7 us -> none  [per_device(): base = space_eigen[:, None] + time_eigen[None, :]]
where the time goes in v2:
time: 149 us; the launch traced here: 148 us
  Pallas kernels  146 us (98%)
    pallas_call x1, Pallas kernels, per_device(): pl.pallas_call(main_kernel, out_shape=(jax.ShapeDtypeStruct(block, F32),...  137 us
    pallas_call x1, Pallas kernels, per_device(): pl.pallas_call(last_kernel, out_shape=(jax.ShapeDtypeStruct(block, F32),)...  9.18 us

profile of v2, /device:TPU:1, one launch (start us, length us, event | category | flops | bytes accessed | tf_op | source)
XLA Modules:
  0.0 148.3 jit_solution(5943090677966647317)
XLA Ops:
  0.6 1.2 reshape.13.se_h
  1.9 137.2 %shard_map.121 = (f32[32,48,384]{2,1,0:T(8,128)}, f32[4608,128]{1,0:T(8,128)}, f32[8,128]{1,0:T(8,128)}) custom-call(f32[32,48,384]{2,1,0:T(8,128)} %r_h.3, f32[32,48,384]{2,1,0:T(8,128)} %d_h.3, f32[32,48,384]{2,1,0:T(8,128)} %reac_h.1, f32[384,384]{1,0:T(8,128)} %s_h.3, f32[512,512]{1,0:T(8,128)} %t_h.1, f32[2,4,384]{2,1,0:T(4,128)} %sb_h.1, ...), custom_call_target="tpu_custom_call" | custom-call | tf_op jit(solution)/shard_map/pallas_call | solution.py:500
  139.1 9.2 %shard_map.122 = (f32[32,48,384]{2,1,0:T(8,128)}, f32[32,48,384]{2,1,0:T(8,128)}, f32[32,48,384]{2,1,0:T(8,128)}) custom-call(f32[4608,128]{1,0:T(8,128)} %get-tuple-element.6.back_h, f32[384,384]{1,0:T(8,128)} %s_h.3, f32[32,48,384]{2,1,0:T(8,128)} %d_h.3, f32[32,48,384]{2,1,0:T(8,128)} %sol_h.1, f32[32,48,384]{2,1,0:T(8,128)} %r_h.3, ...), custom_call_target="tpu_custom_call" | custom-call | tf_op jit(solution)/shard_map/pallas_call | solution.py:530

commit v3 on v2

--- a/solution.py
+++ b/solution.py
@@ -30,10 +30,34 @@
     return z * 4 + (x // 2) * 2 + c, (x % 2) * 4 + y
 
 
-def partner(i, where):
+def wrapped(v):
+    return jnp.where(v >= 4, v - 4, v)
+
+
+def each_partner(where, act):
     z, x, y, c = where
-    a, b, e, d = i % 4, (i // 4) % 4, (i // 16) % 4, i // 64
-    return device((z + a) % 4, (x + a + b) % 4, (y + a + b + e) % 4, (c + d + a) % 2)
+    tops = [wrapped(z + a) * 4 for a in range(4)]
+    cores = [c, 1 - c]
+
+    def outer(b, carry):
+        def inner(e, carry):
+            xb = wrapped(x + b)
+            yb = wrapped(wrapped(y + b) + e)
+            for a in range(4):
+                xa = wrapped(xb + a)
+                high = jnp.where(xa >= 2, 2, 0)
+                s = (xa - high) * 4 + wrapped(yb + a)
+                for d in range(2):
+                    t = tops[a] + high + cores[(a + d) % 2]
+                    if a == 0 and d == 0:
+                        pl.when(b + e > 0)(lambda: act(t, s))
+                    else:
+                        act(t, s)
+            return carry
+
+        return lax.fori_loop(0, 4, inner, carry)
+
+    lax.fori_loop(0, 4, outer, 0)
 
 
 def swap_lanes(pieces):
@@ -130,11 +154,7 @@
 
 
 def send_all(where, copy_to):
-    def body(i, carry):
-        copy_to(*partner(i, where)).start()
-        return carry
-
-    lax.fori_loop(1, 128, body, 0)
+    each_partner(where, lambda t, s: copy_to(t, s).start())
 
 
 def stencil(ext, reac, ycoef, xcoef, tbands, first_t, tcoef, mass, stiff, mixed, rest, image):
@@ -254,11 +274,10 @@
 
     barrier = pltpu.get_barrier_semaphore()
 
-    def greet(i, carry):
-        pl.semaphore_signal(barrier, inc=1, device_id=partner(i, where), device_id_type=MESH)
-        return carry
-
-    lax.fori_loop(1, 128, greet, 0)
+    each_partner(
+        where,
+        lambda t, s: pl.semaphore_signal(barrier, inc=1, device_id=(t, s), device_id_type=MESH),
+    )
     loads[1].wait()
     tripled(left_y, s_v[...].T)
     loads[2].wait()
@@ -285,16 +304,13 @@
     for halo in halos:
         halo.start()
 
-    def piece(ref, d, k):
-        return ref.at[pl.ds(d * ROWS + k * 12, 12)]
-
-    def exchange(n, src, dst, k):
+    def exchange(n, src, dst, start, rows):
         def copy_to(t, s):
             return pltpu.make_async_remote_copy(
-                src_ref=piece(src, t * 8 + s, k),
-                dst_ref=piece(dst, me, k),
-                send_sem=send_sem.at[n * 3 + k],
-                recv_sem=recv_sem.at[n * 3 + k],
+                src_ref=src.at[pl.ds((t * 8 + s) * ROWS + start, rows)],
+                dst_ref=dst.at[pl.ds(me * ROWS + start, rows)],
+                send_sem=send_sem.at[n],
+                recv_sem=recv_sem.at[n],
                 device_id=(t, s),
                 device_id_type=MESH,
             )
@@ -314,8 +330,7 @@
     def own_chunk(src, dst):
         dst[pl.ds(me * ROWS, ROWS), :] = src[pl.ds(me * ROWS, ROWS), :]
 
-    for k in range(3):
-        exchange(0, send1, recv1, k)
+    exchange(0, send1, recv1, 0, ROWS)
     own_chunk(send1, recv1)
 
     loads[3].wait()
@@ -335,8 +350,7 @@
     pack_rows(image, packed)
 
     forward_y(packed, left_y, send2)
-    exchange(1, send2, recv2, 0)
-    exchange(1, send2, recv2, 1)
+    exchange(1, send2, recv2, 0, 24)
     own_chunk(send2, recv2)
 
     for h in range(48):
@@ -363,12 +377,12 @@
         return base_v[...] + seig[k * 128 + me]
 
     def old_part(k, total):
-        finish(k, send1, recv1, 12).wait()
         to_lines(recv1, k, lines)
         v = forward_tx(lines, time_high, time_low, left_x)
         hat_r[pl.ds(pl.multiple_of(k * 384, 384), 384), :] = v
         return total + jnp.sum((v * (v / eigen(k))).reshape(48, 8, 512), axis=0)
 
+    finish(0, send1, recv1, ROWS).wait()
     old = lax.fori_loop(0, 3, old_part, jnp.zeros((8, 512), F32))
     old = old[:, 0:128] + old[:, 128:256] + old[:, 256:384] + old[:, 384:512]
 
@@ -388,17 +402,21 @@
 
     red1s[0:1, :] = jnp.sum(old, axis=0, keepdims=True)
     red1s[1:2, :] = jnp.sum(curve, axis=0, keepdims=True)
-    share(9, red1s, red1, 2)
-    exchange(1, send2, recv2, 2)
-
-    finish(9, red1, red1, 2).wait()
+    share(6, red1s, red1, 2)
+    exchange(2, send2, recv2, 24, 12)
+
+    finish(1, send2, recv2, 24).wait()
+    finish(6, red1, red1, 2).wait()
     every = red1[...]
     even = lax.broadcasted_iota(jnp.int32, (256, 128), 0) % 2 == 0
     norm_old = whole(jnp.where(even, every, 0.0))
     step = norm_old / whole(jnp.where(even, 0.0, every))
 
     def inverse_part(k, total):
-        finish(3 + k, send2, recv2, 12).wait()
+        @pl.when(k == 2)
+        def _():
+            finish(2, send2, recv2, 12).wait()
+
         to_lines(recv2, k, lines)
         rows = pl.ds(pl.multiple_of(k * 384, 384), 384)
         v = hat_r[rows, :] - step * forward_tx(lines, time_high, time_low, left_x)
@@ -410,7 +428,7 @@
             + dot(low, time_high[...], 1, 1)
         )
         to_chunks(lines, k, send1)
-        exchange(2, send1, back_h, k)
+        exchange(3 + k, send1, back_h, k * 12, 12)
         return total + jnp.sum((v * g).reshape(48, 8, 512), axis=0)
 
     new = lax.fori_loop(0, 3, inverse_part, jnp.zeros((8, 512), F32))
@@ -421,8 +439,8 @@
 
     new = new[:, 0:128] + new[:, 128:256] + new[:, 256:384] + new[:, 384:512]
     red2s[...] = jnp.sum(new, axis=0, keepdims=True)
-    share(10, red2s, red2, 1)
-    finish(10, red2, red2, 1).wait()
+    share(7, red2s, red2, 1)
+    finish(7, red2, red2, 1).wait()
     norm_new = whole(red2[...])
     row = lax.broadcasted_iota(jnp.int32, (8, 128), 0)
     scal_o[...] = jnp.where(row == 0, step, norm_new / norm_old)
@@ -430,7 +448,7 @@
     store_image.wait()
     own.wait()
     for k in range(3):
-        finish(6 + k, send1, back_h, 12).wait()
+        finish(3 + k, send1, back_h, 12).wait()
 
 
 def last_kernel(
@@ -518,7 +536,7 @@
             v((38, 3, 64, 128), F32), v((38, 3, 64, 128), F32),
             v((38, 3, 48, 128), F32), v((38, 3, 48, 128), F32),
             v((2, 128), F32), v((256, 128), F32), v((1, 128), F32), v((128, 128), F32),
-            pltpu.SMEM((448,), F32), dma((14,)), dma((8,)), dma((8,)), dma((2,)), dma((11,)), dma((11,)),
+            pltpu.SMEM((448,), F32), dma((14,)), dma((8,)), dma((8,)), dma((2,)), dma((8,)), dma((8,)),
         ],
         compiler_params=pltpu.CompilerParams(
             collective_id=0, has_side_effects=True, vmem_limit_bytes=62 * 2**20

time: 149 us -> 122 us (0.82)
  Pallas kernels: 146 us -> 120 us
    pallas_call x1, Pallas kernels: 137 us -> 111 us  [per_device(): pl.pallas_call(main_kernel, out_shape=(jax.ShapeDtypeStruct(block, F32),...]
where the time goes in v3:
time: 122 us
  Pallas kernels  120 us (98%)
  local copies, waits for them, and re-layouts  1.25 us (1%)
    pallas_call x1, Pallas kernels, per_device(): pl.pallas_call(main_kernel, out_shape=(jax.ShapeDtypeStruct(block, F32),...  111 us
    pallas_call x1, Pallas kernels, per_device(): pl.pallas_call(last_kernel, out_shape=(jax.ShapeDtypeStruct(block, F32),)...  9.2 us

profile of v3, /device:TPU:1, one launch (start us, length us, event | category | flops | bytes accessed | tf_op | source)
XLA Modules:
  0.0 122.1 jit_solution(12608796762352680887)
XLA Ops:
  0.6 1.2 %reshape.13.se_h = f32[1,384]{1,0:T(1,128)} reshape(f32[384]{0:T(512)} %seig.1) | data formatting | bytes 3072 | tf_op jit(solution)/shard_map/reshape | solution.py:546
  1.9 111.0 %shard_map.121 = (f32[32,48,384]{2,1,0:T(8,128)}, f32[4608,128]{1,0:T(8,128)}, f32[8,128]{1,0:T(8,128)}) custom-call(f32[32,48,384]{2,1,0:T(8,128)} %r_h.3, f32[32,48,384]{2,1,0:T(8,128)} %d_h.3, f32[32,48,384]{2,1,0:T(8,128)} %reac_h.1, f32[384,384]{1,0:T(8,128)} %s_h.3, f32[512,512]{1,0:T(8,128)} %t_h.1, f32[2,4,384]{2,1,0:T(4,128)} %sb_h.1, ...), custom_call_target="tpu_custom_call" | custom-call | tf_op jit(solution)/shard_map/pallas_call | solution.py:518
  112.9 9.2 %shard_map.122 = (f32[32,48,384]{2,1,0:T(8,128)}, f32[32,48,384]{2,1,0:T(8,128)}, f32[32,48,384]{2,1,0:T(8,128)}) custom-call(f32[4608,128]{1,0:T(8,128)} %get-tuple-element.6.back_h, f32[384,384]{1,0:T(8,128)} %s_h.3, f32[32,48,384]{2,1,0:T(8,128)} %d_h.3, f32[32,48,384]{2,1,0:T(8,128)} %sol_h.1, f32[32,48,384]{2,1,0:T(8,128)} %r_h.3, ...), custom_call_target="tpu_custom_call" | custom-call | tf_op jit(solution)/shard_map/pallas_call | solution.py:548

commit v4 on v3

--- a/solution.py
+++ b/solution.py
@@ -350,7 +350,8 @@
     pack_rows(image, packed)
 
     forward_y(packed, left_y, send2)
-    exchange(1, send2, recv2, 0, 24)
+    exchange(9, send2, recv2, 0, 12)
+    exchange(10, send2, recv2, 12, 12)
     own_chunk(send2, recv2)
 
     for h in range(48):
@@ -370,7 +371,7 @@
         return carry
 
     lax.fori_loop(0, 32, time_rows, 0)
-    column = jnp.broadcast_to(se_v[...], (8, 384)).T
+    column = jnp.broadcast_to(se_v[...].reshape(1, 384), (8, 384)).T
     base_v[...] = column[:, 0:1] + te_v[...]
 
     def eigen(k):
@@ -403,9 +404,8 @@
     red1s[0:1, :] = jnp.sum(old, axis=0, keepdims=True)
     red1s[1:2, :] = jnp.sum(curve, axis=0, keepdims=True)
     share(6, red1s, red1, 2)
-    exchange(2, send2, recv2, 24, 12)
-
-    finish(1, send2, recv2, 24).wait()
+    exchange(11, send2, recv2, 24, 12)
+
     finish(6, red1, red1, 2).wait()
     every = red1[...]
     even = lax.broadcasted_iota(jnp.int32, (256, 128), 0) % 2 == 0
@@ -413,10 +413,7 @@
     step = norm_old / whole(jnp.where(even, 0.0, every))
 
     def inverse_part(k, total):
-        @pl.when(k == 2)
-        def _():
-            finish(2, send2, recv2, 12).wait()
-
+        finish(9 + k, send2, recv2, 12).wait()
         to_lines(recv2, k, lines)
         rows = pl.ds(pl.multiple_of(k * 384, 384), 384)
         v = hat_r[rows, :] - step * forward_tx(lines, time_high, time_low, left_x)
@@ -457,49 +454,38 @@
     back, s_v, left, d_v, sol_v, r_v, img_v, ns_v, nr_v, nd_v, in_sem, out_sem,
 ):
     start = [pltpu.make_async_copy(s_h, s_v, in_sem.at[0]), pltpu.make_async_copy(back_h, back, in_sem.at[1])]
-    halves = []
-    for half in range(2):
-        t = slice(half * 16, half * 16 + 16)
-        halves.append(
-            [
-                pltpu.make_async_copy(src.at[t], dst.at[t], in_sem.at[2 + half * 4 + n])
-                for n, (src, dst) in enumerate(((d_h, d_v), (sol_h, sol_v), (r_h, r_v), (img_h, img_v)))
-            ]
-        )
-    for copy in start + halves[0] + halves[1]:
+    parts = [(slice(tau * 16, tau * 16 + 16), slice(i * 16, i * 16 + 16)) for tau in range(2) for i in range(3)]
+    loads = [
+        [
+            pltpu.make_async_copy(src.at[t, x], dst.at[t, x], in_sem.at[2 + n * 4 + q])
+            for q, (src, dst) in enumerate(((d_h, d_v), (sol_h, sol_v), (r_h, r_v), (img_h, img_v)))
+        ]
+        for n, (t, x) in enumerate(parts)
+    ]
+    for copy in start + sum(loads, []):
         copy.start()
     start[0].wait()
     tripled(left, s_v[...])
+    step = scal[0:1, 0:1].reshape(1, 1, 1)
+    ratio = scal[1:2, 0:1].reshape(1, 1, 1)
     start[1].wait()
-    step = scal[0:1, 0:1]
-    ratio = scal[1:2, 0:1]
     stores = []
-    for tau in range(2):
-        t = slice(tau * 16, tau * 16 + 16)
-        for copy in halves[tau]:
+    for n, (t, x) in enumerate(parts):
+        lines = []
+        for j in range(2):
+            lines.append(
+                jnp.concatenate([back[pl.ds(k * 12 + n * 2 + j, 128, stride=ROWS), :] for k in range(3)], axis=0)
+            )
+        out = dot(left[...], stacked(jnp.concatenate(lines, axis=1))).T
+        for copy in loads[n]:
             copy.wait()
-
-        def body(i, carry):
-            h = i * 2
-            parts = []
-            for j in range(2):
-                parts.append(
-                    jnp.concatenate(
-                        [back[pl.ds(k * 12 + tau * 6 + h + j, 128, stride=ROWS), :] for k in range(3)], axis=0
-                    )
-                )
-            out = dot(left[...], stacked(jnp.concatenate(parts, axis=1))).T
-            for j in range(2):
-                x = pl.ds(pl.multiple_of((h + j) * 8, 8), 8)
-                d = d_v[t, x, :]
-                nd_v[t, x, :] = out[j * 128 : (j + 1) * 128, :].reshape(16, 8, 384) + ratio.reshape(1, 1, 1) * d
-                ns_v[t, x, :] = sol_v[t, x, :] + step.reshape(1, 1, 1) * d
-                nr_v[t, x, :] = r_v[t, x, :] - step.reshape(1, 1, 1) * img_v[t, x, :]
-            return carry
-
-        lax.fori_loop(0, 3, body, 0)
-        for n, (src, dst) in enumerate(((ns_v, new_sol), (nr_v, new_res), (nd_v, new_dir))):
-            stores.append(pltpu.make_async_copy(src.at[t], dst.at[t], out_sem.at[tau * 3 + n]))
+        ns_v[t, x, :] = sol_v[t, x, :] + step * d_v[t, x, :]
+        nr_v[t, x, :] = r_v[t, x, :] - step * img_v[t, x, :]
+        for j in range(2):
+            part = slice(x.start + j * 8, x.start + j * 8 + 8)
+            nd_v[t, part, :] = out[j * 128 : (j + 1) * 128, :].reshape(16, 8, 384) + ratio * d_v[t, part, :]
+        for q, (src, dst) in enumerate(((ns_v, new_sol), (nr_v, new_res), (nd_v, new_dir))):
+            stores.append(pltpu.make_async_copy(src.at[t, x], dst.at[t, x], out_sem.at[n * 3 + q]))
             stores[-1].start()
     for store in stores:
         store.wait()
@@ -527,7 +513,7 @@
         scratch_shapes=[
             v(block, F32), v((38, 64, 384), F32), v(block, F32), v(block, F32),
             v((384, 384), F32), v((3, 384, 128), F32), v((4, 512, 128), F32), v((2, 4, 384), F32),
-            v((1, 512), F32), v((1, 384), F32), v((384, 512), F32),
+            v((1, 512), F32), v((384,), F32), v((384, 512), F32),
             v((16, 384), F32), v((384, 16), F32), v((14, 48, 128), F32), v((384, 384), F32),
             v((384, 1152), BF16), v((384, 1152), BF16), v((384, 1152), BF16),
             v((512, 512), BF16), v((512, 512), BF16), v((1536, 1152), BF16),
@@ -536,14 +522,14 @@
             v((38, 3, 64, 128), F32), v((38, 3, 64, 128), F32),
             v((38, 3, 48, 128), F32), v((38, 3, 48, 128), F32),
             v((2, 128), F32), v((256, 128), F32), v((1, 128), F32), v((128, 128), F32),
-            pltpu.SMEM((448,), F32), dma((14,)), dma((8,)), dma((8,)), dma((2,)), dma((8,)), dma((8,)),
+            pltpu.SMEM((448,), F32), dma((14,)), dma((8,)), dma((8,)), dma((2,)), dma((12,)), dma((12,)),
         ],
         compiler_params=pltpu.CompilerParams(
             collective_id=0, has_side_effects=True, vmem_limit_bytes=62 * 2**20
         ),
     )(
         residual, direction, reaction, space_basis, time_basis, space_bands,
-        time_eigen.reshape(1, -1), space_eigen.reshape(1, -1), time_bands, space_eigen,
+        time_eigen.reshape(1, -1), space_eigen, time_bands, space_eigen,
     )
     return pl.pallas_call(
         last_kernel,
@@ -553,7 +539,7 @@
         scratch_shapes=[
             v(chunks, F32), v((384, 384), F32), v((384, 1152), BF16),
             *[v(block, F32) for _ in range(7)],
-            dma((10,)), dma((6,)),
+            dma((26,)), dma((18,)),
         ],
         compiler_params=pltpu.CompilerParams(vmem_limit_bytes=62 * 2**20),
     )(back, space_basis, direction, solution, residual, image, scal)

time: 122 us -> 120 us (0.984)
  local copies, waits for them, and re-layouts: 1.25 us -> 0 us
    reshape x1 -> x0, local copies, waits for them, and re-layouts: 1.25 us -> none  [per_device(): space_eigen.reshape(1, -1)]
where the time goes in v4:
time: 120 us
  Pallas kernels  119 us (99%)
    pallas_call x1, Pallas kernels, per_device(): pl.pallas_call(main_kernel, out_shape=(jax.ShapeDtypeStruct(block, F32),...  110 us
    pallas_call x1, Pallas kernels, per_device(): pl.pallas_call(last_kernel, out_shape=(jax.ShapeDtypeStruct(block, F32),)...  8.98 us

profile of v4, /device:TPU:1, one launch (start us, length us, event | category | flops | bytes accessed | tf_op | source)
XLA Modules:
  0.0 119.9 jit_solution(6768613252218691450)
XLA Ops:
  0.6 110.3 %shard_map.121 = (f32[32,48,384]{2,1,0:T(8,128)}, f32[4608,128]{1,0:T(8,128)}, f32[8,128]{1,0:T(8,128)}) custom-call(f32[32,48,384]{2,1,0:T(8,128)} %r_h.3, f32[32,48,384]{2,1,0:T(8,128)} %d_h.3, f32[32,48,384]{2,1,0:T(8,128)} %reac_h.1, f32[384,384]{1,0:T(8,128)} %s_h.3, f32[512,512]{1,0:T(8,128)} %t_h.1, f32[2,4,384]{2,1,0:T(4,128)} %sb_h.1, ...), custom_call_target="tpu_custom_call" | custom-call | tf_op jit(solution)/shard_map/pallas_call | solution.py:504
  110.9 9.0 %shard_map.122 = (f32[32,48,384]{2,1,0:T(8,128)}, f32[32,48,384]{2,1,0:T(8,128)}, f32[32,48,384]{2,1,0:T(8,128)}) custom-call(f32[4608,128]{1,0:T(8,128)} %get-tuple-element.6.back_h, f32[384,384]{1,0:T(8,128)} %s_h.3, f32[32,48,384]{2,1,0:T(8,128)} %d_h.3, f32[32,48,384]{2,1,0:T(8,128)} %sol_h.1, f32[32,48,384]{2,1,0:T(8,128)} %r_h.3, ...), custom_call_target="tpu_custom_call" | custom-call | tf_op jit(solution)/shard_map/pallas_call | solution.py:534
